TPU v7x, 128 devices: a whole 4x4x4 slice. The times are simulated.
128 devices in a mesh: fsdp: 8 (over z_lo, x), tp: 16 (over y, z_hi, core).
Axes of the slice: x: 4, y: 4, z: 4 (z_hi: 2, z_lo: 2; z = z_hi * 2 + z_lo), core: 2. Of those that a mesh axis runs over, the one named last changes fastest.
Arguments:
- ref_gate: bfloat16 [6144, 11008], P('fsdp', 'tp'), may hold values from -6 to 6
- ref_up: bfloat16 [6144, 11008], P('fsdp', 'tp'), may hold values from -6 to 6
- ref_residual: bfloat16 [6144, 4096], P('fsdp', 'tp'), may hold values from -6 to 6
- ref_modality: int32 [6144], P('fsdp'), may hold values 0 or 1
- ref_down_text: bfloat16 [4096, 11008], P('fsdp', 'tp'), may hold values from -0.0546875 to 0.0546875
- ref_down_image: bfloat16 [4096, 11008], P('fsdp', 'tp'), may hold values from -0.0546875 to 0.0546875
- pol_gate: bfloat16 [6144, 11008], P('fsdp', 'tp'), may hold values from -6 to 6
- pol_up: bfloat16 [6144, 11008], P('fsdp', 'tp'), may hold values from -6 to 6
- pol_modality: int32 [6144], P('fsdp'), may hold values 0 or 1
- pol_segment: int32 [6144], P('fsdp'), may hold values from 0 to 11, never falling along the last dimension, each value on 1 to 768 neighbouring positions
- pair_margin: float32 [6], replicated, may hold values from -30 to 30
- token_cotangent: bfloat16 [6144, 4096], P('fsdp', 'tp'), may hold values from -24 to 24
- pol_down_text: bfloat16 [4096, 11008], P('fsdp', 'tp'), may hold values from -0.0546875 to 0.0546875
- pol_down_image: bfloat16 [4096, 11008], P('fsdp', 'tp'), may hold values from -0.0546875 to 0.0546875
Outputs:
- ref_out: bfloat16 [6144, 4096], P('fsdp', 'tp')
- grad_gate: bfloat16 [6144, 11008], P('fsdp', 'tp')
- grad_up: bfloat16 [6144, 11008], P('fsdp', 'tp')
- grad_down_text: float32 [4096, 11008], P('fsdp', 'tp')
- grad_down_image: float32 [4096, 11008], P('fsdp', 'tp')
Inputs may be any that keep to these rules, and one draw needn't show every extreme that they name: `ref_modality`: 0 marks a text token, 1 an image token. `pol_modality`: 0 marks a text token, 1 an image token. `pol_segment`: response numbers never fall along the tokens; responses 2p and 2p + 1 are the chosen and the rejected response of pair p; every response has at least one token.
All inputs are finite; a program needn't handle non-finite values. No bound on the sum of `ref_modality` or of `pol_modality` on one device may be relied on, other than what follows from the above.
Results may differ from a plain program's by a relative error of at most 0.015.
Values may be sent and summed in bfloat16 or wider, within the bound.
A program may use at most 128 MiB of HBM per device.

v0:
```python
import jax
import jax.numpy as jnp
from jax import lax
from jax.sharding import PartitionSpec as P

dpo_beta = 0.1


def sent_together(arrays, axis, dim, along):
    ends, at = ([], 0)
    for a in arrays[:-1]:
        at += a.shape[along]
        ends.append(at)
    both = jnp.concatenate(arrays, axis=along)
    return tuple(jnp.split(lax.all_gather(both, axis, axis=dim, tiled=True), ends, axis=along))


def split_hidden(gate, up, modality):
    gate_f = gate.astype(jnp.float32)
    up_f = up.astype(jnp.float32)
    sig = jax.nn.sigmoid(gate_f)
    act = gate_f * sig
    hidden = (act * up_f).astype(jnp.bfloat16)
    image = (modality == 1)[:, None]
    zero = jnp.zeros_like(hidden)
    return (jnp.where(image, zero, hidden), jnp.where(image, hidden, zero), gate_f, up_f, sig, act)


def forward_term(left_text, left_image, right_text, right_image):
    contract = (((1,), (1,)), ((), ()))
    part = lax.dot_general(left_text, right_text, contract, preferred_element_type=jnp.float32)
    return part + lax.dot_general(
        left_image, right_image, contract, preferred_element_type=jnp.float32
    )


def backward_term(left_text, left_image, right_text, right_image):
    part = jnp.dot(left_text, right_text, preferred_element_type=jnp.float32)
    return part + jnp.dot(left_image, right_image, preferred_element_type=jnp.float32)


def per_device(
    ref_gate,
    ref_up,
    ref_residual,
    ref_modality,
    ref_down_text,
    ref_down_image,
    pol_gate,
    pol_up,
    pol_modality,
    pol_segment,
    pair_margin,
    token_cotangent,
    pol_down_text,
    pol_down_image,
):
    ref_text, ref_image, _, _, _, _ = split_hidden(ref_gate, ref_up, ref_modality)
    pol_text, pol_image, gate_f, up_f, sig, act = split_hidden(pol_gate, pol_up, pol_modality)
    seg_ids = jnp.arange(2 * pair_margin.shape[0], dtype=jnp.int32)
    pair_weight = dpo_beta * jax.nn.sigmoid(-dpo_beta * pair_margin)
    table = jnp.repeat(pair_weight, 2) * jnp.where(seg_ids % 2 == 0, -1.0, 1.0).astype(jnp.float32)
    coef = jnp.sum(
        jnp.where(pol_segment[:, None] == seg_ids[None, :], table[None, :], jnp.float32(0.0)),
        axis=1,
    )
    local_cot = (coef[:, None] * token_cotangent.astype(jnp.float32)).astype(jnp.bfloat16)
    full_cot = lax.all_gather(local_cot, "tp", axis=1, tiled=True)
    image_p = (pol_modality == 1)[:, None]
    zero_cot = jnp.zeros_like(full_cot)
    cot_text = jnp.where(image_p, zero_cot, full_cot)
    cot_image = jnp.where(image_p, full_cot, zero_cot)
    whole_rt, whole_ri, whole_pt, whole_pi = sent_together(
        (ref_down_text, ref_down_image, pol_down_text, pol_down_image), "fsdp", 0, 1
    )
    terms = forward_term(ref_text, ref_image, whole_rt, whole_ri)
    d_hidden = backward_term(cot_text, cot_image, whole_pt, whole_pi)
    summed = lax.psum_scatter(
        terms.astype(jnp.bfloat16), "tp", scatter_dimension=1, tiled=True
    ).astype(jnp.float32)
    ref_out = (summed + ref_residual.astype(jnp.float32)).astype(jnp.bfloat16)
    grad_gate = (d_hidden * up_f * sig * (1.0 + gate_f * (1.0 - sig))).astype(jnp.bfloat16)
    grad_up = (d_hidden * act).astype(jnp.bfloat16)
    width = pol_down_text.shape[1]
    over_rows = (((0,), (0,)), ((), ()))
    term_text = lax.dot_general(cot_text, pol_text, over_rows, preferred_element_type=jnp.float32)
    term_image = lax.dot_general(
        cot_image, pol_image, over_rows, preferred_element_type=jnp.float32
    )
    grads = lax.psum_scatter(
        jnp.concatenate([term_text, term_image], axis=1).astype(jnp.bfloat16),
        "fsdp",
        scatter_dimension=0,
        tiled=True,
    ).astype(jnp.float32)
    return (ref_out, grad_gate, grad_up, grads[:, :width], grads[:, width:])


def solution(mesh):
    in_specs = (
        P("fsdp", "tp"),
        P("fsdp", "tp"),
        P("fsdp", "tp"),
        P("fsdp"),
        P("fsdp", "tp"),
        P("fsdp", "tp"),
        P("fsdp", "tp"),
        P("fsdp", "tp"),
        P("fsdp"),
        P("fsdp"),
        P(),
        P("fsdp", "tp"),
        P("fsdp", "tp"),
        P("fsdp", "tp"),
    )
    out_specs = (
        P("fsdp", "tp"),
        P("fsdp", "tp"),
        P("fsdp", "tp"),
        P("fsdp", "tp"),
        P("fsdp", "tp"),
    )
    return jax.shard_map(
        per_device, mesh=mesh, in_specs=in_specs, out_specs=out_specs, check_vma=False
    )
```

profile of v0, /device:TPU:2, one launch (start us, length us, event | category | flops | bytes accessed | tf_op | source)
XLA Modules:
  0.0 528.9 jit_solution(288210245870872746)
XLA Ops:
  7.2 0.0 all-gather.5.cloned.1.call-start
  7.2 0.7 divide_multiply_fusion
  7.9 0.1 broadcast_in_dim.66
  7.9 0.1 reshape.33
  8.0 0.8 select_reduce_fusion
  8.8 1.9 multiply_convert_fusion.1
  10.7 0.0 all-gather.5.cloned.1.call-update
  10.8 0.0 all-gather.3.cloned.1.call-start
  10.8 3.0 pad_maximum_fusion.1
  13.8 0.0 copy-start.1
  13.8 0.0 copy-start.6
  13.8 0.0 copy-start.7
  13.8 0.0 all-gather.3.cloned.1.call-update
  13.9 0.0 reduce-scatter.5.cloned.1.call-start
  13.9 0.6 copy-done.1
  14.5 67.6 %all-gather.5.cloned.1.call-done = bf16[768,4096]{1,0:T(8,128)(2,1)} async-done(((bf16[768,256]{1,0:T(8,128)(2,1)}), bf16[768,4096]{1,0:T(8,128)(2,1)}) %all-gather.5.cloned.1.call-update) | async-done | bytes 6291472 | tf_op jit(solution)/shard_map/all_gather | solution.py:68
  82.1 0.0 copy-done.6
  82.1 0.0 copy-done.7
  82.1 0.0 copy-start.3
  82.1 8.2 %convolution_convert_fusion = bf16[4096,688]{0,1:T(8,128)(2,1)S(1)} fusion(bf16[768,4096]{1,0:T(8,128)(2,1)} %all-gather.5.cloned.1.call-done, pred[768]{0:T(1024)(128)(4,1)S(1)} %broadcast_compare_fusion, bf16[768,688]{0,1:T(8,128)(2,1)S(1)} %copy-done.6, bf16[768,688]{0,1:T(8,128)(2,1)S(1)} %copy-done.7), kind=kOutput, calls=%fused_computation.2 | convolution fusion | flops 4339240960 | bytes 14041856 | tf_op jit(solution)/shard_map/dot_general | solution.py:87
  90.3 0.0 copy-done.3
  90.3 5.3 %convolution_convert_fusion.1 = bf16[4096,688]{0,1:T(8,128)(2,1)S(1)} fusion(bf16[768,4096]{1,0:T(8,128)(2,1)S(1)} %copy-done.3, pred[768]{0:T(1024)(128)(4,1)S(1)} %broadcast_compare_fusion, bf16[768,688]{0,1:T(8,128)(2,1)S(1)} %copy-done.6, bf16[768,688]{0,1:T(8,128)(2,1)S(1)} %copy-done.7), kind=kOutput, calls=%fused_computation.3 | convolution fusion | flops 4339240960 | bytes 14041856 | tf_op jit(solution)/shard_map/dot_general | solution.py:86
  95.6 10.4 %pad_maximum_fusion = bf16[4096,1376]{0,1:T(8,128)(2,1)} fusion(bf16[4096,688]{0,1:T(8,128)(2,1)S(1)} %convolution_convert_fusion, bf16[4096,688]{0,1:T(8,128)(2,1)S(1)} %convolution_convert_fusion.1), kind=kLoop, calls=%fused_computation.1 | loop fusion | flops 22544384 | bytes 22544384 | tf_op jit(solution)/shard_map/concatenate | solution.py:91
  106.0 0.0 copy-start.2
  106.0 0.0 copy-start.4
  106.0 0.0 reduce-scatter.5.cloned.1.call-update
  106.1 0.2 reduce-scatter.3.cloned.1.call-start
  106.3 0.4 copy-done.2
  106.7 197.7 %all-gather.3.cloned.1.call-done = bf16[4096,2752]{0,1:T(8,128)(2,1)} async-done(((bf16[512,2752]{0,1:T(8,128)(2,1)}), bf16[4096,2752]{0,1:T(8,128)(2,1)}) %all-gather.3.cloned.1.call-update) | async-done | bytes 22544400 | tf_op jit(solution)/shard_map/all_gather | solution.py:15
  304.4 0.0 copy-done.4
  304.4 0.0 copy-done.5
  304.4 7.6 %fusion.5 = f32[768,4096]{1,0:T(8,128)S(1)} fusion(bf16[4096,2752]{0,1:T(8,128)(2,1)} %all-gather.3.cloned.1.call-done, pred[768]{0:T(1024)(128)(4,1)S(1)} %broadcast_compare_fusion.1, bf16[768,688]{0,1:T(8,128)(2,1)S(1)} %copy-done.4, bf16[768,688]{0,1:T(8,128)(2,1)S(1)} %copy-done.5), kind=kOutput, calls=%fused_computation.11 | convolution fusion | flops 4333277184 | bytes 20333312 | tf_op jit(solution)/shard_map/dot_general | solution.py:31
  312.1 10.2 %add_convert_fusion = bf16[768,4096]{1,0:T(8,128)(2,1)} fusion(f32[768,4096]{1,0:T(8,128)S(1)} %fusion.5, bf16[4096,2752]{0,1:T(8,128)(2,1)} %all-gather.3.cloned.1.call-done, pred[768]{0:T(1024)(128)(4,1)S(1)} %broadcast_compare_fusion.1, bf16[768,688]{0,1:T(8,128)(2,1)S(1)} %copy-done.4, bf16[768,688]{0,1:T(8,128)(2,1)S(1)} %copy-done.5), kind=kOutput, calls=%fused_computation | convolution fusion | flops 4339568640 | bytes 26624768 | tf_op jit(solution)/shard_map/dot_general | solution.py:32
  322.3 0.0 reduce-scatter.3.cloned.1.call-update
  322.3 103.3 %reduce-scatter.5.cloned.1.call-done = bf16[512,1376]{0,1:T(8,128)(2,1)} async-done(((bf16[4096,1376]{0,1:T(8,128)(2,1)}), bf16[512,1376]{0,1:T(8,128)(2,1)}) %reduce-scatter.5.cloned.1.call-update) | async-done | bytes 1409040 | tf_op jit(solution)/shard_map/reduce_scatter | solution.py:90
  425.6 0.0 slice-start
  425.6 3.4 fusion.46
  429.0 0.0 slice-start.1
  429.0 0.0 copy-start.8
  429.0 8.8 %fusion = f32[768,688]{0,1:T(8,128)S(1)} fusion(bf16[4096,2752]{0,1:T(8,128)(2,1)} %all-gather.3.cloned.1.call-done, bf16[768,4096]{1,0:T(8,128)(2,1)} %all-gather.5.cloned.1.call-done, pred[768]{0:T(1024)(128)(4,1)S(1)} %broadcast_compare_fusion), kind=kOutput, calls=%fused_computation.6 | convolution fusion | flops 4331667456 | bytes 14041856 | tf_op jit(solution)/shard_map/dot_general | solution.py:39
  437.9 0.0 slice-done
  437.9 0.0 slice-done.1
  437.9 0.0 copy-done.8
  437.9 0.0 copy-start
  437.9 9.7 %multiply_convert_fusion = (bf16[768,688]{0,1:T(8,128)(2,1)}, bf16[768,688]{0,1:T(8,128)(2,1)}) fusion(bf16[768,688]{0,1:T(8,128)(2,1)S(1)} %copy-done.8, bf16[768,688]{0,1:T(8,128)(2,1)S(1)} %copy-done.6, f32[768,688]{0,1:T(8,128)S(1)} %fusion, bf16[4096,2752]{0,1:T(8,128)(2,1)} %all-gather.3.cloned.1.call-done, bf16[768,4096]{1,0:T(8,128)(2,1)S(1)} %bitcast.1, ...), kind=kOutput, calls=%fused_computation.33 | convolution fusion | flops 4340121600 | bytes 18268928 | tf_op jit(solution)/shard_map/dot_general | solution.py:38
  447.6 72.9 %reduce-scatter.3.cloned.1.call-done = bf16[768,256]{1,0:T(8,128)(2,1)} async-done(((bf16[768,4096]{1,0:T(8,128)(2,1)}), bf16[768,256]{1,0:T(8,128)(2,1)}) %reduce-scatter.3.cloned.1.call-update) | async-done | bytes 393232 | tf_op jit(solution)/shard_map/reduce_scatter | solution.py:78
  520.5 0.0 copy-done
  520.5 1.8 add_convert_fusion.1
  (5 shorter events, 0.0 us)
Async XLA Ops:
  7.2 74.9 %all-gather.5.cloned.1.call-start = ((), (), s32[]{:S(2)}) async-start(), calls=%async_computation.4 | async-start | bytes 6684672 | tf_op jit(solution)/shard_map/all_gather | solution.py:68
  10.8 293.7 %all-gather.3.cloned.1.call-start = ((), (), s32[]{:S(2)}) async-start(), calls=%async_computation.2 | async-start | bytes 25362432 | tf_op jit(solution)/shard_map/all_gather | solution.py:15
  13.8 0.7 copy-start.1
  13.8 68.3 %copy-start.6 = (bf16[768,688]{0,1:T(8,128)(2,1)S(1)}, bf16[768,688]{0,1:T(8,128)(2,1)}, u32[]{:S(2)}) copy-start(bf16[768,688]{0,1:T(8,128)(2,1)} %param.21) | copy-start | bytes 3170308
  13.8 68.3 %copy-start.7 = (bf16[768,688]{0,1:T(8,128)(2,1)S(1)}, bf16[768,688]{0,1:T(8,128)(2,1)}, u32[]{:S(2)}) copy-start(bf16[768,688]{0,1:T(8,128)(2,1)} %param.20) | copy-start | bytes 3170308
  13.9 411.8 %reduce-scatter.5.cloned.1.call-start = ((), (), s32[]{:S(2)}) async-start(), calls=%async_computation.5 | async-start | bytes 12681216 | tf_op jit(solution)/shard_map/reduce_scatter | solution.py:90
  82.1 8.2 %copy-start.3 = (bf16[768,4096]{1,0:T(8,128)(2,1)S(1)}, bf16[768,4096]{1,0:T(8,128)(2,1)}, u32[]{:S(2)}) copy-start(bf16[768,4096]{1,0:T(8,128)(2,1)} %all-gather.5.cloned.1.call-done) | copy-start | bytes 18874372
  106.0 0.7 copy-start.2
  106.0 198.4 %copy-start.4 = (bf16[768,688]{0,1:T(8,128)(2,1)S(1)}, bf16[768,688]{0,1:T(8,128)(2,1)}, u32[]{:S(2)}) copy-start(bf16[768,688]{0,1:T(8,128)(2,1)} %param.15) | copy-start | bytes 3170308
  106.0 198.4 %copy-start.5 = (bf16[768,688]{0,1:T(8,128)(2,1)S(1)}, bf16[768,688]{0,1:T(8,128)(2,1)}, u32[]{:S(2)}) copy-start(bf16[768,688]{0,1:T(8,128)(2,1)} %param.14) | copy-start | bytes 3170308
  106.1 414.4 %reduce-scatter.3.cloned.1.call-start = ((), (), s32[]{:S(2)}) async-start(), calls=%async_computation.3 | async-start | bytes 6684672 | tf_op jit(solution)/shard_map/reduce_scatter | solution.py:78
  425.6 12.2 %slice-start = ((s8[6291456]{0:T(1024)(128)(4,1)}), s8[4194304]{0:T(1024)(128)(4,1)S(1)}, s32[]{:S(2)}) async-start(s8[6291456]{0:T(1024)(128)(4,1)} %bitcast), calls=%async_computation.6 | async-start | bytes 8388608
  429.0 8.8 %slice-start.1 = ((s8[6291456]{0:T(1024)(128)(4,1)}), s8[2097152]{0:T(1024)(128)(4,1)S(1)}, s32[]{:S(2)}) async-start(s8[6291456]{0:T(1024)(128)(4,1)} %bitcast), calls=%async_computation.7 | async-start | bytes 4194304
  429.0 8.8 %copy-start.8 = (bf16[768,688]{0,1:T(8,128)(2,1)S(1)}, bf16[768,688]{0,1:T(8,128)(2,1)}, u32[]{:S(2)}) copy-start(bf16[768,688]{0,1:T(8,128)(2,1)} %param.20) | copy-start | bytes 3170308
  437.9 82.6 %copy-start = (bf16[768,256]{1,0:T(8,128)(2,1)S(1)}, bf16[768,256]{1,0:T(8,128)(2,1)}, u32[]{:S(2)}) copy-start(bf16[768,256]{1,0:T(8,128)(2,1)} %param.16) | copy-start | bytes 1179652
Sparse Core Ops, SparseCore 0:
  10.9 71.1 all-gather.4
  83.7 220.6 all-gather.2
  306.9 118.6 reduce-scatter.4
  429.6 90.8 reduce-scatter.2
where the time goes:
time: 529 us
  waiting for transfers between devices  442 us (84%)
  matrix products  49.8 us (9%)
  other arithmetic  18.6 us (4%)
  between operations  13.9 us (3%)
    all_gather x1, waiting for transfers between devices, sent_together(): lax.all_gather(both, axis, axis=dim, tiled=True)  198 us
    reduce_scatter x1, waiting for transfers between devices, per_device(): lax.psum_scatter(jnp.concatenate([term_text, term_image], axis=1).astype(...  103 us
    reduce_scatter x1, waiting for transfers between devices, per_device(): lax.psum_scatter(terms.astype(jnp.bfloat16), 'tp', scatter_dimension=1, t...  72.9 us
    all_gather x1, waiting for transfers between devices, per_device(): full_cot = lax.all_gather(local_cot, 'tp', axis=1, tiled=True)  67.6 us
  transfers between devices with their start and end apart: 4, of which 4 were waited for; matrix products, arithmetic and copies ran while one was open for 13% of the time, Pallas kernels for 0%

commit v1 on v0

v1 whole, which is shorter than its diff:
```python
import jax
import jax.numpy as jnp
from jax import lax
from jax.experimental import pallas as pl
from jax.experimental.pallas import tpu as pltpu
from jax.sharding import PartitionSpec as P

dpo_beta = 0.1
bf16 = jnp.bfloat16
f32 = jnp.float32
MESH = pl.DeviceIdType.MESH


N_SEM = 48


def lanes(n, width=256):
    return pl.ds(pl.multiple_of(n * width, width), width)


def loop(count, body):
    def step(n, carry):
        body(n)
        return carry

    lax.fori_loop(0, count, step, 0)


def step_kernel(
    cot_in,
    mod_in,
    href_in,
    wref_in,
    hpol_in,
    wpol_in,
    out_ref,
    out_d,
    out_w,
    hr,
    hp,
    wr,
    wp,
    cr,
    mods,
    hs,
    cs,
    aw,
    ar,
    kp,
    sr,
    va,
    vb,
    ga,
    gb,
    za,
    zr,
    fo,
    dh,
    xa_via,
    xb_via,
    xa,
    xb,
    dws,
    dwr,
    send_sems,
    recv_sems,
    local_sems,
):
    fi = lax.axis_index("fsdp")
    ti = lax.axis_index("tp")
    zl, x = fi // 4, fi % 4
    y, zh, c = ti // 4, (ti // 2) % 2, ti % 2
    ff, rows = href_in.shape
    cols = cot_in.shape[0]
    cut = (ff // 32) * 16
    tiles = rows // 256

    def device(x2, zl2, y2, zh2, c2):
        return (zl2 * 4 + x2, y2 * 4 + zh2 * 2 + c2)

    x_up, x_down = device((x + 1) % 4, zl, y, zh, c), device((x + 3) % 4, zl, y, zh, c)
    x_opp = device((x + 2) % 4, zl, y, zh, c)
    y_up, y_down = device(x, zl, (y + 1) % 4, zh, c), device(x, zl, (y + 3) % 4, zh, c)
    zl_flip, zh_flip = device(x, 1 - zl, y, zh, c), device(x, zl, y, 1 - zh, c)
    c_flip = device(x, zl, y, zh, 1 - c)
    rows_x = (y % 2) * 2 + zh
    rows_d = (x - rows_x + 4) % 4
    rows_y = ((y // 2 + zl) % 2) * 2 + rows_d // 2
    rows_dev = device(rows_x, zl, rows_y, rows_d % 2, c)
    rows_k = rows_y * 2 + rows_d % 2
    back_d = (y % 2) * 2 + zh
    back_dev = device((x + back_d) % 4, zl, ((y // 2 + zl) % 2) * 2 + x // 2, x % 2, c)
    stays = jnp.logical_and(rows_dev[0] == fi, rows_dev[1] == ti)
    moves = jnp.logical_not(stays)

    barrier = pltpu.get_barrier_semaphore()
    for dev in (x_up, x_down, x_opp, y_up, y_down, zl_flip, zh_flip, c_flip):
        pl.semaphore_signal(barrier, inc=1, device_id=dev, device_id_type=MESH)

    @pl.when(moves)
    def _():
        for dev in (rows_dev, back_dev):
            pl.semaphore_signal(barrier, inc=1, device_id=dev, device_id_type=MESH)

    pl.semaphore_wait(barrier, jnp.where(moves, 10, 8))

    started = []

    def copy(src, dst, dev):
        n = len(started)
        rdma = pltpu.make_async_remote_copy(
            src_ref=src,
            dst_ref=dst,
            send_sem=send_sems.at[n],
            recv_sem=recv_sems.at[n],
            device_id=dev,
            device_id_type=MESH,
        )
        started.append(rdma)
        rdma.start()
        return rdma

    def copy_or_stay(n, src, dst, dst_here, dev):
        rdma = pltpu.make_async_remote_copy(
            src_ref=src,
            dst_ref=dst,
            send_sem=send_sems.at[n],
            recv_sem=recv_sems.at[n],
            device_id=dev,
            device_id_type=MESH,
        )
        here = pltpu.make_async_copy(src, dst_here, local_sems.at[n - N_SEM])

        @pl.when(moves)
        def _():
            rdma.start()

        @pl.when(stays)
        def _():
            here.start()

        def wait():
            @pl.when(moves)
            def _():
                rdma.wait()

            @pl.when(stays)
            def _():
                here.wait()

        return wait

    def local(n, src, dst):
        here = pltpu.make_async_copy(src, dst, local_sems.at[n])
        here.start()
        return here

    k_own = y * 2 + zh
    wait_moved = copy_or_stay(N_SEM, cot_in, cr.at[c, rows_k], cr.at[c, k_own], rows_dev)
    m_up = copy(mod_in, mods.at[3], x_up)
    m_down = copy(mod_in, mods.at[1], x_down)
    m_opp = copy(mod_in, mods.at[2], x_opp)
    h_up = copy(href_in, hr.at[3], x_up)
    h_down = copy(href_in, hr.at[1], x_down)
    half = wref_in.shape[0] // 2
    w_lo = copy(wref_in.at[pl.ds(0, half)], wr.at[1, pl.ds(0, half)], zl_flip)
    own = [
        local(2, mod_in, mods.at[0]),
        local(3, href_in, hr.at[0]),
        local(4, wref_in, wr.at[0]),
        local(5, hpol_in, hp.at[0]),
        local(6, wpol_in, wp.at[0]),
    ]

    wait_moved()
    cot_zh = copy(cr.at[c, k_own], cr.at[c, k_own], zh_flip)
    w_hi = copy(wref_in.at[pl.ds(half, half)], wr.at[1, pl.ds(half, half)], zl_flip)
    for here in own:
        here.wait()
    cot_zh.wait_recv()
    pair = cr.at[c, pl.ds(y * 2, 2)]
    cot_up = copy(pair, pair, y_up)
    cot_down = copy(pair, pair, y_down)
    wp_far = copy(wpol_in, wp.at[1], zl_flip)
    cot_c = [copy(pair, pair, c_flip)]

    h_up.wait_recv()
    h_down.wait_recv()
    lo, hi = pl.ds(0, cut), pl.ds(cut, ff - cut)
    h_opp_lo = copy(hr.at[3, lo], hr.at[2, lo], x_up)
    h_opp_hi = copy(hr.at[1, hi], hr.at[2, hi], x_down)
    p_up = copy(hpol_in, hp.at[3], x_up)
    p_down = copy(hpol_in, hp.at[1], x_down)
    m_up.wait_recv()
    m_down.wait_recv()
    m_opp.wait_recv()

    below, above, opp = (y + 3) % 4, (y + 1) % 4, (y + 2) % 4

    def image(d, row, where):
        return mods[d, pl.ds(row, 1), where].astype(bf16)

    def ref_piece(d, slot):
        def tile(n):
            where = lanes(n)
            img = image(d, 0, where)
            block = hr[d, :, where]
            hs[pl.ds(0, ff)] = block * (1 - img)
            hs[pl.ds(ff, ff)] = block * img
            for r in range(2):
                there = pl.ds(pl.multiple_of((1 - c) * cols, cols), cols)
                away = jnp.dot(wr[r, there], hs[...], preferred_element_type=f32)
                aw[d, r, :, where] = away.astype(bf16)
                stay = pl.ds(pl.multiple_of(c * cols, cols), cols)
                kp[slot, r, :, where] = jnp.dot(wr[r, stay], hs[...], preferred_element_type=f32)

        loop(tiles, tile)
        return copy(aw.at[d], ar.at[d], c_flip)

    def ref_sum(d, slot, got):
        got.wait_recv()

        def tile(n):
            where = lanes(n)
            for r in range(2):
                total = kp[slot, r, :, where] + ar[d, r, :, where].astype(f32)
                sr[r * 4 + d, :, where] = total.astype(bf16)

        loop(tiles, tile)

    w_lo.wait_recv()
    w_hi.wait_recv()
    got0 = ref_piece(0, 0)

    cot_up.wait_recv()
    cot_down.wait_recv()
    cot_opp_lo = copy(cr.at[c, below * 2], cr.at[c, below * 2], y_up)
    cot_opp_hi = copy(cr.at[c, above * 2 + 1], cr.at[c, above * 2 + 1], y_down)
    for at in (below, above):
        other = cr.at[c, pl.ds(at * 2, 2)]
        cot_c.append(copy(other, other, c_flip))

    got1 = ref_piece(1, 1)
    ref_sum(0, 0, got0)
    got3 = ref_piece(3, 0)
    ref_sum(1, 1, got1)
    h_opp_lo.wait_recv()
    h_opp_hi.wait_recv()
    got2 = ref_piece(2, 1)
    ref_sum(3, 0, got3)
    ref_sum(2, 1, got2)

    via_up = copy(sr.at[opp * 2], va, y_up)
    via_down = copy(sr.at[opp * 2 + 1], vb, y_down)
    first_up = copy(sr.at[above * 2 + 1], ga.at[1], y_up)
    first_down = copy(sr.at[below * 2], gb.at[0], y_down)

    cot_opp_lo.wait_recv()
    cot_opp_hi.wait_recv()
    other = cr.at[c, pl.ds(opp * 2, 2)]
    cot_c.append(copy(other, other, c_flip))

    p_up.wait_recv()
    p_down.wait_recv()
    p_opp_lo = copy(hp.at[3, lo], hp.at[2, lo], x_up)
    p_opp_hi = copy(hp.at[1, hi], hp.at[2, hi], x_down)

    via_up.wait_recv()
    via_down.wait_recv()

    def add_via(n):
        where = lanes(n)
        for at, via in ((above * 2, va), (below * 2 + 1, vb)):
            total = sr[at, :, where].astype(f32) + via[:, where].astype(f32)
            sr[at, :, where] = total.astype(bf16)

    loop(tiles, add_via)
    last_up = copy(sr.at[above * 2], ga.at[0], y_up)
    last_down = copy(sr.at[below * 2 + 1], gb.at[1], y_down)

    for got in cot_c:
        got.wait_recv()
    wp_far.wait_recv()

    def d_piece(d, store):
        def tile(n):
            where = lanes(n)
            img = image(d, 1, where)
            for r in range(2):
                for core in range(2):
                    block = cr[core, r * 4 + d, :, where]
                    at = r * 4 * cols + core * cols
                    cs[pl.ds(at, cols)] = block * (1 - img)
                    cs[pl.ds(at + 2 * cols, cols)] = block * img
            part = jnp.dot(wp[0], cs[pl.ds(0, 4 * cols)], preferred_element_type=f32)
            part += jnp.dot(wp[1], cs[pl.ds(4 * cols, 4 * cols)], preferred_element_type=f32)
            store(where, part)

        loop(tiles, tile)

    def store_dh(slot):
        def store(where, part):
            dh[slot, :, where] = part.astype(bf16)

        return store

    d_piece(2, store_dh(2))
    d_via_up = copy(dh.at[2, lo], xa_via, x_up)
    d_via_down = copy(dh.at[2, hi], xb_via, x_down)

    first_up.wait_recv()
    first_down.wait_recv()
    last_up.wait_recv()
    last_down.wait_recv()

    def y_sum(k, where):
        total = sr[y * 2 + k, :, where].astype(f32) + ga[k, :, where].astype(f32)
        return total + gb[k, :, where].astype(f32)

    def z_away(n):
        where = lanes(n)
        za[:, where] = y_sum(1 - zh, where).astype(bf16)

    loop(tiles, z_away)
    z_copy = copy(za, zr, zh_flip)

    p_opp_lo.wait_recv()
    p_opp_hi.wait_recv()

    def down(r, core, modality):
        total = None
        for d in range(4):
            img = image(d, 1, slice(None))
            block = cr[core, r * 4 + d] * (img if modality else 1 - img)
            part = lax.dot_general(
                hp[d], block, (((1,), (1,)), ((), ())), preferred_element_type=f32
            )
            total = part if total is None else total + part
        return total

    d_piece(1, store_dh(0))
    d_first_up = copy(dh.at[0, hi], xa.at[hi], x_up)
    d_piece(3, store_dh(1))
    d_first_down = copy(dh.at[1, lo], xb.at[lo], x_down)

    dw_sent = []
    for modality in range(2):

        def away(core, modality=modality):
            dws[modality, :, lanes(core)] = down(1, core, modality).astype(bf16)

        loop(2, away)
        dw_sent.append(copy(dws.at[modality], dwr.at[modality], zl_flip))

    d_via_up.wait_recv()
    d_via_down.wait_recv()

    def add_d(n):
        where = lanes(n)
        dh[0, lo, where] = (dh[0, lo, where].astype(f32) + xa_via[:, where].astype(f32)).astype(bf16)
        dh[1, hi, where] = (dh[1, hi, where].astype(f32) + xb_via[:, where].astype(f32)).astype(bf16)

    loop(tiles, add_d)
    d_last_up = copy(dh.at[0, lo], xa.at[lo], x_up)
    d_last_down = copy(dh.at[1, hi], xb.at[hi], x_down)

    z_copy.wait_recv()

    def z_sum(n):
        where = lanes(n)
        fo[:, where] = (y_sum(zh, where) + zr[:, where].astype(f32)).astype(bf16)

    loop(tiles, z_sum)
    wait_back = copy_or_stay(N_SEM + 1, fo, out_ref, out_ref, back_dev)

    def store_own(where, part):
        out_d[:, where] = part

    d_piece(0, store_own)

    for modality in range(2):
        for core in range(2):
            out_w[modality, :, pl.ds(core * cols, cols)] = down(0, core, modality)

    for got in (d_first_up, d_first_down, d_last_up, d_last_down):
        got.wait_recv()

    def d_sum(n):
        where = lanes(n)
        both = xa[:, where].astype(f32) + xb[:, where].astype(f32)
        out_d[:, where] = out_d[:, where] + both

    loop(tiles, d_sum)
    for modality in range(2):
        dw_sent[modality].wait_recv()

        def dw_sum(core, modality=modality):
            where = lanes(core)
            out_w[modality, :, where] = out_w[modality, :, where] + dwr[modality, :, where].astype(f32)

        loop(2, dw_sum)
    wait_back()
    for rdma in started:
        rdma.wait_send()


def communicate(cot, mod, href, wref, hpol, wpol):
    ff, rows = href.shape
    cols = cot.shape[0]
    depth = wref.shape[0]
    cut = (ff // 32) * 16
    vmem = pltpu.VMEM
    scratch = [
        vmem((4, ff, rows), bf16),
        vmem((4, ff, rows), bf16),
        vmem((2, depth, 2 * ff), bf16),
        vmem((2, ff, 2 * depth), bf16),
        vmem((2, 8, cols, rows), bf16),
        vmem((4, 8, rows), f32),
        vmem((2 * ff, 256), bf16),
        vmem((8 * cols, 256), bf16),
        vmem((4, 2, cols, rows), bf16),
        vmem((4, 2, cols, rows), bf16),
        vmem((2, 2, cols, rows), f32),
        vmem((8, cols, rows), bf16),
        vmem((cols, rows), bf16),
        vmem((cols, rows), bf16),
        vmem((2, cols, rows), bf16),
        vmem((2, cols, rows), bf16),
        vmem((cols, rows), bf16),
        vmem((cols, rows), bf16),
        vmem((cols, rows), bf16),
        vmem((3, ff, rows), bf16),
        vmem((cut, rows), bf16),
        vmem((ff - cut, rows), bf16),
        vmem((ff, rows), bf16),
        vmem((ff, rows), bf16),
        vmem((2, ff, depth), bf16),
        vmem((2, ff, depth), bf16),
        pltpu.SemaphoreType.DMA((N_SEM + 2,)),
        pltpu.SemaphoreType.DMA((N_SEM + 2,)),
        pltpu.SemaphoreType.DMA((8,)),
    ]
    anywhere = pl.BlockSpec(memory_space=pl.ANY)
    in_vmem = pl.BlockSpec(memory_space=vmem)
    return pl.pallas_call(
        step_kernel,
        out_shape=(
            jax.ShapeDtypeStruct((cols, rows), bf16),
            jax.ShapeDtypeStruct((ff, rows), f32),
            jax.ShapeDtypeStruct((2, ff, depth), f32),
        ),
        in_specs=[anywhere] * 6,
        out_specs=(in_vmem,) * 3,
        scratch_shapes=scratch,
        compiler_params=pltpu.CompilerParams(
            collective_id=0, has_side_effects=True, vmem_limit_bytes=66_000_000
        ),
    )(cot, mod, href, wref, hpol, wpol)


def per_device(
    ref_gate,
    ref_up,
    ref_residual,
    ref_modality,
    ref_down_text,
    ref_down_image,
    pol_gate,
    pol_up,
    pol_modality,
    pol_segment,
    pair_margin,
    token_cotangent,
    pol_down_text,
    pol_down_image,
):
    rows = ref_gate.shape[0]
    seg_ids = jnp.arange(2 * pair_margin.shape[0], dtype=jnp.int32)
    pair_weight = dpo_beta * jax.nn.sigmoid(-dpo_beta * pair_margin)
    table = jnp.repeat(pair_weight, 2) * jnp.where(seg_ids % 2 == 0, -1.0, 1.0).astype(f32)
    coef = jnp.sum(
        jnp.where(pol_segment[None, :] == seg_ids[:, None], table[:, None], f32(0.0)), axis=0
    )
    cot = (coef[None, :] * token_cotangent.T.astype(f32)).astype(bf16)
    mod = jnp.stack([ref_modality == 1, pol_modality == 1]).astype(f32)
    mod = jnp.concatenate([mod, jnp.zeros((6, rows), f32)], axis=0)

    gate_r = ref_gate.T.astype(f32)
    h_ref = (gate_r * jax.nn.sigmoid(gate_r) * ref_up.T.astype(f32)).astype(bf16)
    gate_p, up_p = pol_gate.T.astype(f32), pol_up.T.astype(f32)
    sig = jax.nn.sigmoid(gate_p)
    act = gate_p * sig
    h_pol = (act * up_p).astype(bf16)
    w_ref = jnp.concatenate([ref_down_text, ref_down_image], axis=1)
    w_pol = jnp.concatenate([pol_down_text.T, pol_down_image.T], axis=1)

    summed, d_hidden, grads = communicate(cot, mod, h_ref, w_ref, h_pol, w_pol)
    ref_out = (summed.T.astype(f32) + ref_residual.astype(f32)).astype(bf16)
    grad_gate = (d_hidden * up_p * sig * (1.0 + gate_p * (1.0 - sig))).astype(bf16)
    grad_up = (d_hidden * act).astype(bf16)
    return (ref_out, grad_gate.T, grad_up.T, grads[0].T, grads[1].T)


def solution(mesh):
    spec = P("fsdp", "tp")
    in_specs = (
        spec,
        spec,
        spec,
        P("fsdp"),
        spec,
        spec,
        spec,
        spec,
        P("fsdp"),
        P("fsdp"),
        P(),
        spec,
        spec,
        spec,
    )
    return jax.shard_map(
        per_device, mesh=mesh, in_specs=in_specs, out_specs=(spec,) * 5, check_vma=False
    )
```

time: 529 us -> 171 us (0.32)
  waiting for transfers between devices: 442 us -> 0 us
  Pallas kernels: 0 us -> 151 us
  matrix products: 49.8 us -> 0 us
  between operations: 13.9 us -> 0.86 us
  other arithmetic: 18.6 us -> 11.8 us
    all_gather x2 -> x0, waiting for transfers between devices: 265 us -> none  [the longest x1 198 us: sent_together(): lax.all_gather(both, axis, axis=dim, tiled=True)]
    reduce_scatter x2 -> x0, waiting for transfers between devices: 176 us -> none  [the longest x1 103 us: per_device(): lax.psum_scatter(jnp.concatenate([term_text, term_image], axis=1).astype(...]
    pallas_call x0 -> x1, Pallas kernels: none -> 151 us  [communicate(): pl.pallas_call(step_kernel, out_shape=(jax.ShapeDtypeStruct((cols, rows),...]
    dot_general x6 -> x0, matrix products: 49.8 us -> none  [the longest x1 10.2 us: forward_term(): lax.dot_general(left_image, right_image, contract, preferred_element_type...]
    concatenate x2 -> x3, other arithmetic: 13.4 us -> 3.51 us  [the longest x1 1.59 us: per_device(): w_ref = jnp.concatenate([ref_down_text, ref_down_image], axis=1)]
  transfers between devices with their start and end apart: 4 -> 0, of which waited for: 4 -> 0; matrix products, arithmetic and copies ran while one was open for 13% -> 0% of each run, Pallas kernels for 0% -> 0%
where the time goes in v1:
time: 171 us; the launch traced here: 169 us
  Pallas kernels  151 us (88%)
  other arithmetic  11.8 us (7%)
  local copies, waits for them, and re-layouts  5.8 us (3%)
    pallas_call x1, Pallas kernels, communicate(): pl.pallas_call(step_kernel, out_shape=(jax.ShapeDtypeStruct((cols, rows),...  151 us
    convert_element_type x1, other arithmetic, per_device(): h_pol = (act * up_p).astype(bf16)  4.89 us
    transpose x1, local copies, waits for them, and re-layouts, per_device(): return (ref_out, grad_gate.T, grad_up.T, grads[0].T, grads[1].T)  3.75 us

profile of v1, /device:TPU:2, one launch (start us, length us, event | category | flops | bytes accessed | tf_op | source)
XLA Modules:
  0.0 169.1 jit_solution(16037655616138732550)
XLA Ops:
  0.6 0.0 copy-start.3
  0.6 0.0 copy-start.4
  0.7 4.9 %fusion = (bf16[688,768]{1,0:T(8,128)(2,1)}, bf16[688,768]{1,0:T(8,128)(2,1)}) fusion(bf16[768,688]{0,1:T(8,128)(2,1)} %param.21, bf16[768,688]{0,1:T(8,128)(2,1)} %param.20, bf16[768,688]{0,1:T(8,128)(2,1)} %param.15, bf16[768,688]{0,1:T(8,128)(2,1)} %param.14), kind=kLoop, calls=%fused_computation.2 | loop fusion | flops 8454144 | bytes 6340608 | tf_op jit(solution)/shard_map/convert_element_type | solution.py:494
  5.5 0.0 copy-done.3
  5.5 0.3 copy.30
  5.8 0.0 copy-done.4
  5.8 0.0 copy-start.5
  5.8 0.3 copy.31
  6.1 0.0 copy-start.6
  6.1 1.6 pad_maximum_fusion.wref_in
  7.7 0.0 copy-start.7
  7.7 0.0 copy-start.13
  7.7 0.0 copy-start.12
  7.7 0.0 copy-done.5
  7.7 0.0 copy-done.6
  7.8 0.0 copy-start.10
  7.8 0.0 copy-start.11
  7.8 1.3 pad_maximum_fusion.1.wpol_in
  9.1 0.0 copy-done.7
  9.1 0.2 copy.29
  9.3 0.0 copy-done.13
  9.3 0.1 broadcast_in_dim.28
  9.4 0.1 reshape.31
  9.4 0.0 copy-done.12
  9.5 0.1 select_reduce_fusion
  9.5 0.8 fusion.15.cot_in
  10.4 0.0 copy-done.10
  10.4 0.0 copy-done.11
  10.4 0.6 pad_convert_fusion.mod_in
  11.0 150.6 %shard_map.173 = (bf16[256,768]{1,0:T(8,128)(2,1)}, f32[688,768]{1,0:T(8,128)}, f32[2,688,512]{2,1,0:T(8,128)}) custom-call(bf16[256,768]{1,0:T(8,128)(2,1)} %fusion.15.cot_in, f32[8,768]{1,0:T(8,128)} %pad_convert_fusion.mod_in, bf16[688,768]{1,0:T(8,128)(2,1)} %get-tuple-element.31.href_in, bf16[512,1376]{1,0:T(8,128)(2,1)} %pad_maximum_fusion.wref_in, ...), custom_call_target="tpu_custom_call" | custom-call | tf_op jit(solution)/shard_map/pallas_call | solution.py:446
  161.6 0.0 copy-start
  161.6 0.0 copy-start.1
  161.7 0.0 copy-start.2
  161.7 3.8 %slice_bitcast_fusion = (f32[512,688]{0,1:T(8,128)}, f32[512,688]{0,1:T(8,128)}) fusion(f32[2,688,512]{2,1,0:T(8,128)} %get-tuple-element.10), kind=kLoop, calls=%fused_computation.23 | loop fusion | bytes 5636096 | tf_op jit(solution)/shard_map/transpose | solution.py:502
  165.4 0.0 copy-done
  165.4 0.0 copy-done.1
  165.4 0.0 copy-done.2
  165.4 0.0 copy-start.8
  165.4 0.0 copy-start.9
  165.5 2.4 %fusion.12 = (bf16[768,688]{0,1:T(8,128)(2,1)}, bf16[768,688]{0,1:T(8,128)(2,1)}) fusion(f32[688,768]{1,0:T(8,128)S(1)} %copy-done.2, bf16[768,688]{0,1:T(8,128)(2,1)S(1)} %copy-done.1, bf16[768,688]{0,1:T(8,128)(2,1)S(1)} %copy-done), kind=kLoop, calls=%fused_computation.25 | loop fusion | flops 7925760 | bytes 6340608 | tf_op jit(solution)/shard_map/transpose | solution.py:502
  167.8 0.0 copy-done.8
  167.9 0.2 copy.32
  168.0 0.0 copy-done.9
  168.0 0.1 fusion.14
  168.1 0.9 copy.33
  (7 shorter events, 0.1 us)
Async XLA Ops:
  0.6 4.9 %copy-start.3 = (bf16[512,688]{0,1:T(8,128)(2,1)S(1)}, bf16[512,688]{0,1:T(8,128)(2,1)}, u32[]{:S(2)}) copy-start(bf16[512,688]{0,1:T(8,128)(2,1)} %param.18) | copy-start | bytes 2113540
  0.6 5.2 %copy-start.4 = (bf16[512,688]{0,1:T(8,128)(2,1)S(1)}, bf16[512,688]{0,1:T(8,128)(2,1)}, u32[]{:S(2)}) copy-start(bf16[512,688]{0,1:T(8,128)(2,1)} %param.19) | copy-start | bytes 2113540
  5.8 1.9 %copy-start.5 = (bf16[512,688]{0,1:T(8,128)(2,1)S(1)}, bf16[512,688]{0,1:T(8,128)(2,1)}, u32[]{:S(2)}) copy-start(bf16[512,688]{0,1:T(8,128)(2,1)} %param.27) | copy-start | bytes 2113540
  6.1 1.6 copy-start.6
  7.7 1.4 copy-start.7
  7.7 1.5 copy-start.13
  7.7 1.7 %copy-start.12 = (s32[768]{0:T(1024)S(1)}, s32[768]{0:T(1024)}, u32[]{:S(2)}) copy-start(s32[768]{0:T(1024)} %param.23) | copy-start | bytes 9220
  7.8 2.6 %copy-start.10 = (s32[768]{0:T(1024)S(1)}, s32[768]{0:T(1024)}, u32[]{:S(2)}) copy-start(s32[768]{0:T(1024)} %param.22) | copy-start | bytes 9220
  7.8 2.6 %copy-start.11 = (s32[768]{0:T(1024)S(1)}, s32[768]{0:T(1024)}, u32[]{:S(2)}) copy-start(s32[768]{0:T(1024)} %param.17) | copy-start | bytes 9220
  161.6 3.8 %copy-start = (bf16[768,688]{0,1:T(8,128)(2,1)S(1)}, bf16[768,688]{0,1:T(8,128)(2,1)}, u32[]{:S(2)}) copy-start(bf16[768,688]{0,1:T(8,128)(2,1)} %param.21) | copy-start | bytes 3170308
  161.6 3.8 %copy-start.1 = (bf16[768,688]{0,1:T(8,128)(2,1)S(1)}, bf16[768,688]{0,1:T(8,128)(2,1)}, u32[]{:S(2)}) copy-start(bf16[768,688]{0,1:T(8,128)(2,1)} %param.20) | copy-start | bytes 3170308
  161.7 3.8 %copy-start.2 = (f32[688,768]{1,0:T(8,128)S(1)}, f32[688,768]{1,0:T(8,128)}, u32[]{:S(2)}) copy-start(f32[688,768]{1,0:T(8,128)} %get-tuple-element.9) | copy-start | bytes 6340612
  165.4 2.4 %copy-start.8 = (bf16[768,256]{1,0:T(8,128)(2,1)S(1)}, bf16[768,256]{1,0:T(8,128)(2,1)}, u32[]{:S(2)}) copy-start(bf16[768,256]{1,0:T(8,128)(2,1)} %param.16) | copy-start | bytes 1179652
  165.4 2.6 %copy-start.9 = (bf16[256,768]{1,0:T(8,128)(2,1)S(1)}, bf16[256,768]{1,0:T(8,128)(2,1)}, u32[]{:S(2)}) copy-start(bf16[256,768]{1,0:T(8,128)(2,1)} %get-tuple-element.8) | copy-start | bytes 1179652

commit v2 on v1

--- a/solution.py
+++ b/solution.py
@@ -11,7 +11,7 @@
 MESH = pl.DeviceIdType.MESH
 
 
-N_SEM = 48
+N_SEM = 64
 
 
 def lanes(n, width=256):
@@ -29,13 +29,21 @@
 def step_kernel(
     cot_in,
     mod_in,
-    href_in,
+    gate_r_in,
+    up_r_in,
+    gate_p_in,
+    up_p_in,
     wref_in,
-    hpol_in,
-    wpol_in,
+    wpol_t_in,
+    wpol_i_in,
     out_ref,
-    out_d,
-    out_w,
+    out_gate,
+    out_up,
+    out_t,
+    out_i,
+    gates,
+    turned,
+    d_own,
     hr,
     hp,
     wr,
@@ -70,7 +78,7 @@
     ti = lax.axis_index("tp")
     zl, x = fi // 4, fi % 4
     y, zh, c = ti // 4, (ti // 2) % 2, ti % 2
-    ff, rows = href_in.shape
+    ff, rows = gate_r_in.shape
     cols = cot_in.shape[0]
     cut = (ff // 32) * 16
     tiles = rows // 256
@@ -87,11 +95,30 @@
     rows_d = (x - rows_x + 4) % 4
     rows_y = ((y // 2 + zl) % 2) * 2 + rows_d // 2
     rows_dev = device(rows_x, zl, rows_y, rows_d % 2, c)
-    rows_k = rows_y * 2 + rows_d % 2
+    turn_dev = device(x, zl, rows_y, rows_d % 2, c)
     back_d = (y % 2) * 2 + zh
     back_dev = device((x + back_d) % 4, zl, ((y // 2 + zl) % 2) * 2 + x // 2, x % 2, c)
-    stays = jnp.logical_and(rows_dev[0] == fi, rows_dev[1] == ti)
-    moves = jnp.logical_not(stays)
+    moves = jnp.logical_or(rows_dev[0] != fi, rows_dev[1] != ti)
+    turn_x = (x - back_d + 4) % 4
+    turn_src = device(x, zl, ((y // 2 + zl) % 2) * 2 + turn_x // 2, turn_x % 2, c)
+    turns = turn_dev[1] != ti
+    shift_dev = device(turn_x, zl, y, zh, c)
+    shifts = back_d != 0
+
+    def local(n, src, dst):
+        here = pltpu.make_async_copy(src, dst, local_sems.at[n])
+        here.start()
+        return here
+
+    ref_here = [local(3, gate_r_in, gates.at[0]), local(4, up_r_in, gates.at[1])]
+    depth = wpol_t_in.shape[1]
+    pol_here = [local(5, gate_p_in, gates.at[2]), local(6, up_p_in, gates.at[3])]
+    own = [
+        local(7, mod_in, mods.at[0]),
+        local(8, wref_in, wr.at[0]),
+        local(9, wpol_t_in, wp.at[0, :, pl.ds(0, depth)]),
+        local(10, wpol_i_in, wp.at[0, :, pl.ds(depth, depth)]),
+    ]
 
     barrier = pltpu.get_barrier_semaphore()
     for dev in (x_up, x_down, x_opp, y_up, y_down, zl_flip, zh_flip, c_flip):
@@ -102,7 +129,23 @@
         for dev in (rows_dev, back_dev):
             pl.semaphore_signal(barrier, inc=1, device_id=dev, device_id_type=MESH)
 
-    pl.semaphore_wait(barrier, jnp.where(moves, 10, 8))
+    @pl.when(turns)
+    def _():
+        for dev in (turn_dev, turn_src):
+            pl.semaphore_signal(barrier, inc=1, device_id=dev, device_id_type=MESH)
+
+    def hidden(first, out):
+        def chunk(n):
+            where = pl.ds(pl.multiple_of(n * 16, 16), 16)
+            gate, up = gates[first, where].astype(f32), gates[first + 1, where].astype(f32)
+            out[0, where] = (gate * jax.nn.sigmoid(gate) * up).astype(bf16)
+
+        loop(ff // 16, chunk)
+
+    for here in ref_here:
+        here.wait()
+    hidden(0, hr)
+    pl.semaphore_wait(barrier, 8 + jnp.where(moves, 2, 0) + jnp.where(turns, 2, 0))
 
     started = []
 
@@ -120,7 +163,7 @@
         rdma.start()
         return rdma
 
-    def copy_or_stay(n, src, dst, dst_here, dev):
+    def copy_or_stay(n, src, dst, dev, moves):
         rdma = pltpu.make_async_remote_copy(
             src_ref=src,
             dst_ref=dst,
@@ -129,7 +172,8 @@
             device_id=dev,
             device_id_type=MESH,
         )
-        here = pltpu.make_async_copy(src, dst_here, local_sems.at[n - N_SEM])
+        here = pltpu.make_async_copy(src, dst, local_sems.at[n - N_SEM])
+        stays = jnp.logical_not(moves)
 
         @pl.when(moves)
         def _():
@@ -150,52 +194,65 @@
 
         return wait
 
-    def local(n, src, dst):
-        here = pltpu.make_async_copy(src, dst, local_sems.at[n])
-        here.start()
-        return here
-
+    below, above, opp = (y + 3) % 4, (y + 1) % 4, (y + 2) % 4
+    lo, hi = pl.ds(0, cut), pl.ds(cut, ff - cut)
     k_own = y * 2 + zh
-    wait_moved = copy_or_stay(N_SEM, cot_in, cr.at[c, rows_k], cr.at[c, k_own], rows_dev)
+    wait_turned = copy_or_stay(N_SEM, cot_in, turned, turn_dev, turns)
     m_up = copy(mod_in, mods.at[3], x_up)
     m_down = copy(mod_in, mods.at[1], x_down)
     m_opp = copy(mod_in, mods.at[2], x_opp)
-    h_up = copy(href_in, hr.at[3], x_up)
-    h_down = copy(href_in, hr.at[1], x_down)
-    half = wref_in.shape[0] // 2
-    w_lo = copy(wref_in.at[pl.ds(0, half)], wr.at[1, pl.ds(0, half)], zl_flip)
-    own = [
-        local(2, mod_in, mods.at[0]),
-        local(3, href_in, hr.at[0]),
-        local(4, wref_in, wr.at[0]),
-        local(5, hpol_in, hp.at[0]),
-        local(6, wpol_in, wp.at[0]),
-    ]
-
+
+    def spread_first(h):
+        return copy(h.at[0, lo], h.at[3, lo], x_up), copy(h.at[0, hi], h.at[1, hi], x_down)
+
+    def spread_last(h):
+        return copy(h.at[0, hi], h.at[3, hi], x_up), copy(h.at[0, lo], h.at[1, lo], x_down)
+
+    def pass_on(h, up_first, down_first):
+        up_first.wait_recv()
+        down_first.wait_recv()
+        return copy(h.at[3, lo], h.at[2, lo], x_up), copy(h.at[1, hi], h.at[2, hi], x_down)
+
+    h_up, h_down = spread_first(hr)
+    some = wref_in.shape[0] // 4
+    w_far = []
+
+    def send_w(first, count):
+        where = pl.ds(first * some, count * some)
+        w_far.append(copy(wref_in.at[where], wr.at[1, where], zl_flip))
+
+    send_w(0, 2)
+    for here in pol_here:
+        here.wait()
+    hidden(2, hp)
+
+    wait_turned()
+    wait_moved = copy_or_stay(N_SEM + 2, turned, cr.at[c, k_own], shift_dev, shifts)
+    h_up2, h_down2 = spread_last(hr)
+    h_opp_lo, h_opp_hi = pass_on(hr, h_up, h_down)
+    p_up, p_down = spread_first(hp)
+    p_up2, p_down2 = spread_last(hp)
     wait_moved()
-    cot_zh = copy(cr.at[c, k_own], cr.at[c, k_own], zh_flip)
-    w_hi = copy(wref_in.at[pl.ds(half, half)], wr.at[1, pl.ds(half, half)], zl_flip)
+    cot_zh = [copy(cr.at[c, k_own], cr.at[c, k_own], zh_flip)]
+    send_w(2, 1)
     for here in own:
         here.wait()
-    cot_zh.wait_recv()
+    send_w(3, 1)
+    wp_far = [
+        copy(wpol_t_in, wp.at[1, :, pl.ds(0, depth)], zl_flip),
+        copy(wpol_i_in, wp.at[1, :, pl.ds(depth, depth)], zl_flip),
+    ]
+    for got in cot_zh:
+        got.wait_recv()
     pair = cr.at[c, pl.ds(y * 2, 2)]
     cot_up = copy(pair, pair, y_up)
     cot_down = copy(pair, pair, y_down)
-    wp_far = copy(wpol_in, wp.at[1], zl_flip)
     cot_c = [copy(pair, pair, c_flip)]
-
-    h_up.wait_recv()
-    h_down.wait_recv()
-    lo, hi = pl.ds(0, cut), pl.ds(cut, ff - cut)
-    h_opp_lo = copy(hr.at[3, lo], hr.at[2, lo], x_up)
-    h_opp_hi = copy(hr.at[1, hi], hr.at[2, hi], x_down)
-    p_up = copy(hpol_in, hp.at[3], x_up)
-    p_down = copy(hpol_in, hp.at[1], x_down)
     m_up.wait_recv()
     m_down.wait_recv()
     m_opp.wait_recv()
-
-    below, above, opp = (y + 3) % 4, (y + 1) % 4, (y + 2) % 4
+    h_up2.wait_recv()
+    h_down2.wait_recv()
 
     def image(d, row, where):
         return mods[d, pl.ds(row, 1), where].astype(bf16)
@@ -228,10 +285,14 @@
 
         loop(tiles, tile)
 
-    w_lo.wait_recv()
-    w_hi.wait_recv()
+    for got in w_far:
+        got.wait_recv()
     got0 = ref_piece(0, 0)
-
+    p_opp_lo, p_opp_hi = pass_on(hp, p_up, p_down)
+    got1 = ref_piece(1, 1)
+    ref_sum(0, 0, got0)
+    got3 = ref_piece(3, 0)
+    ref_sum(1, 1, got1)
     cot_up.wait_recv()
     cot_down.wait_recv()
     cot_opp_lo = copy(cr.at[c, below * 2], cr.at[c, below * 2], y_up)
@@ -239,11 +300,6 @@
     for at in (below, above):
         other = cr.at[c, pl.ds(at * 2, 2)]
         cot_c.append(copy(other, other, c_flip))
-
-    got1 = ref_piece(1, 1)
-    ref_sum(0, 0, got0)
-    got3 = ref_piece(3, 0)
-    ref_sum(1, 1, got1)
     h_opp_lo.wait_recv()
     h_opp_hi.wait_recv()
     got2 = ref_piece(2, 1)
@@ -259,28 +315,6 @@
     cot_opp_hi.wait_recv()
     other = cr.at[c, pl.ds(opp * 2, 2)]
     cot_c.append(copy(other, other, c_flip))
-
-    p_up.wait_recv()
-    p_down.wait_recv()
-    p_opp_lo = copy(hp.at[3, lo], hp.at[2, lo], x_up)
-    p_opp_hi = copy(hp.at[1, hi], hp.at[2, hi], x_down)
-
-    via_up.wait_recv()
-    via_down.wait_recv()
-
-    def add_via(n):
-        where = lanes(n)
-        for at, via in ((above * 2, va), (below * 2 + 1, vb)):
-            total = sr[at, :, where].astype(f32) + via[:, where].astype(f32)
-            sr[at, :, where] = total.astype(bf16)
-
-    loop(tiles, add_via)
-    last_up = copy(sr.at[above * 2], ga.at[0], y_up)
-    last_down = copy(sr.at[below * 2 + 1], gb.at[1], y_down)
-
-    for got in cot_c:
-        got.wait_recv()
-    wp_far.wait_recv()
 
     def d_piece(d, store):
         def tile(n):
@@ -304,29 +338,6 @@
 
         return store
 
-    d_piece(2, store_dh(2))
-    d_via_up = copy(dh.at[2, lo], xa_via, x_up)
-    d_via_down = copy(dh.at[2, hi], xb_via, x_down)
-
-    first_up.wait_recv()
-    first_down.wait_recv()
-    last_up.wait_recv()
-    last_down.wait_recv()
-
-    def y_sum(k, where):
-        total = sr[y * 2 + k, :, where].astype(f32) + ga[k, :, where].astype(f32)
-        return total + gb[k, :, where].astype(f32)
-
-    def z_away(n):
-        where = lanes(n)
-        za[:, where] = y_sum(1 - zh, where).astype(bf16)
-
-    loop(tiles, z_away)
-    z_copy = copy(za, zr, zh_flip)
-
-    p_opp_lo.wait_recv()
-    p_opp_hi.wait_recv()
-
     def down(r, core, modality):
         total = None
         for d in range(4):
@@ -338,19 +349,59 @@
             total = part if total is None else total + part
         return total
 
+    def away(modality):
+        def column(core):
+            dws[modality, :, lanes(core)] = down(1, core, modality).astype(bf16)
+
+        loop(2, column)
+
+    for got in cot_c:
+        got.wait_recv()
+    for got in wp_far:
+        got.wait_recv()
+    d_piece(2, store_dh(2))
+    d_via_up = copy(dh.at[2, lo], xa_via, x_up)
+    d_via_down = copy(dh.at[2, hi], xb_via, x_down)
+    p_up2.wait_recv()
+    p_down2.wait_recv()
+    p_opp_lo.wait_recv()
+    p_opp_hi.wait_recv()
+    away(0)
+    dw_sent = [copy(dws.at[0], dwr.at[0], zl_flip)]
+    via_up.wait_recv()
+    via_down.wait_recv()
+
+    def add_via(n):
+        where = lanes(n)
+        for at, via in ((above * 2, va), (below * 2 + 1, vb)):
+            total = sr[at, :, where].astype(f32) + via[:, where].astype(f32)
+            sr[at, :, where] = total.astype(bf16)
+
+    loop(tiles, add_via)
+    last_up = copy(sr.at[above * 2], ga.at[0], y_up)
+    last_down = copy(sr.at[below * 2 + 1], gb.at[1], y_down)
+
     d_piece(1, store_dh(0))
     d_first_up = copy(dh.at[0, hi], xa.at[hi], x_up)
     d_piece(3, store_dh(1))
     d_first_down = copy(dh.at[1, lo], xb.at[lo], x_down)
 
-    dw_sent = []
-    for modality in range(2):
-
-        def away(core, modality=modality):
-            dws[modality, :, lanes(core)] = down(1, core, modality).astype(bf16)
-
-        loop(2, away)
-        dw_sent.append(copy(dws.at[modality], dwr.at[modality], zl_flip))
+    first_up.wait_recv()
+    first_down.wait_recv()
+    last_up.wait_recv()
+    last_down.wait_recv()
+
+    def y_sum(k, where):
+        total = sr[y * 2 + k, :, where].astype(f32) + ga[k, :, where].astype(f32)
+        return total + gb[k, :, where].astype(f32)
+
+    def z_away(n):
+        where = lanes(n)
+        za[:, where] = y_sum(1 - zh, where).astype(bf16)
+
+    loop(tiles, z_away)
+    z_copy = [copy(za, zr, zh_flip)]
+    away(1)
 
     d_via_up.wait_recv()
     d_via_down.wait_recv()
@@ -363,40 +414,48 @@
     loop(tiles, add_d)
     d_last_up = copy(dh.at[0, lo], xa.at[lo], x_up)
     d_last_down = copy(dh.at[1, hi], xb.at[hi], x_down)
-
-    z_copy.wait_recv()
+    dw_sent.append(copy(dws.at[1], dwr.at[1], zl_flip))
+
+    def store_own(where, part):
+        d_own[:, where] = part
+
+
+    d_piece(0, store_own)
+    for got in z_copy:
+        got.wait_recv()
 
     def z_sum(n):
         where = lanes(n)
         fo[:, where] = (y_sum(zh, where) + zr[:, where].astype(f32)).astype(bf16)
 
     loop(tiles, z_sum)
-    wait_back = copy_or_stay(N_SEM + 1, fo, out_ref, out_ref, back_dev)
-
-    def store_own(where, part):
-        out_d[:, where] = part
-
-    d_piece(0, store_own)
-
-    for modality in range(2):
-        for core in range(2):
-            out_w[modality, :, pl.ds(core * cols, cols)] = down(0, core, modality)
+    wait_back = copy_or_stay(N_SEM + 1, fo, out_ref, back_dev, moves)
+
+    for modality, out in enumerate((out_t, out_i)):
+
+        def column(core, modality=modality, out=out):
+            out[:, lanes(core)] = down(0, core, modality)
+
+        loop(2, column)
 
     for got in (d_first_up, d_first_down, d_last_up, d_last_down):
         got.wait_recv()
 
     def d_sum(n):
-        where = lanes(n)
-        both = xa[:, where].astype(f32) + xb[:, where].astype(f32)
-        out_d[:, where] = out_d[:, where] + both
-
-    loop(tiles, d_sum)
-    for modality in range(2):
+        where = pl.ds(pl.multiple_of(n * 16, 16), 16)
+        gate, up = gates[2, where].astype(f32), gates[3, where].astype(f32)
+        d_hidden = d_own[where] + xa[where].astype(f32) + xb[where].astype(f32)
+        sig = jax.nn.sigmoid(gate)
+        out_gate[where] = (d_hidden * up * sig * (1.0 + gate * (1.0 - sig))).astype(bf16)
+        out_up[where] = (d_hidden * (gate * sig)).astype(bf16)
+
+    loop(ff // 16, d_sum)
+    for modality, out in enumerate((out_t, out_i)):
         dw_sent[modality].wait_recv()
 
-        def dw_sum(core, modality=modality):
+        def dw_sum(core, modality=modality, out=out):
             where = lanes(core)
-            out_w[modality, :, where] = out_w[modality, :, where] + dwr[modality, :, where].astype(f32)
+            out[:, where] = out[:, where] + dwr[modality, :, where].astype(f32)
 
         loop(2, dw_sum)
     wait_back()
@@ -404,13 +463,16 @@
         rdma.wait_send()
 
 
-def communicate(cot, mod, href, wref, hpol, wpol):
-    ff, rows = href.shape
+def communicate(cot, mod, gate_r, up_r, gate_p, up_p, wref, wpol_t, wpol_i):
+    ff, rows = gate_r.shape
     cols = cot.shape[0]
     depth = wref.shape[0]
     cut = (ff // 32) * 16
     vmem = pltpu.VMEM
     scratch = [
+        vmem((4, ff, rows), bf16),
+        vmem((cols, rows), bf16),
+        vmem((ff, rows), f32),
         vmem((4, ff, rows), bf16),
         vmem((4, ff, rows), bf16),
         vmem((2, depth, 2 * ff), bf16),
@@ -437,9 +499,9 @@
         vmem((ff, rows), bf16),
         vmem((2, ff, depth), bf16),
         vmem((2, ff, depth), bf16),
-        pltpu.SemaphoreType.DMA((N_SEM + 2,)),
-        pltpu.SemaphoreType.DMA((N_SEM + 2,)),
-        pltpu.SemaphoreType.DMA((8,)),
+        pltpu.SemaphoreType.DMA((N_SEM + 3,)),
+        pltpu.SemaphoreType.DMA((N_SEM + 3,)),
+        pltpu.SemaphoreType.DMA((11,)),
     ]
     anywhere = pl.BlockSpec(memory_space=pl.ANY)
     in_vmem = pl.BlockSpec(memory_space=vmem)
@@ -447,16 +509,18 @@
         step_kernel,
         out_shape=(
             jax.ShapeDtypeStruct((cols, rows), bf16),
-            jax.ShapeDtypeStruct((ff, rows), f32),
-            jax.ShapeDtypeStruct((2, ff, depth), f32),
+            jax.ShapeDtypeStruct((ff, rows), bf16),
+            jax.ShapeDtypeStruct((ff, rows), bf16),
+            jax.ShapeDtypeStruct((ff, depth), f32),
+            jax.ShapeDtypeStruct((ff, depth), f32),
         ),
-        in_specs=[anywhere] * 6,
-        out_specs=(in_vmem,) * 3,
+        in_specs=[anywhere] * 9,
+        out_specs=(in_vmem,) * 5,
         scratch_shapes=scratch,
         compiler_params=pltpu.CompilerParams(
             collective_id=0, has_side_effects=True, vmem_limit_bytes=66_000_000
         ),
-    )(cot, mod, href, wref, hpol, wpol)
+    )(cot, mod, gate_r, up_r, gate_p, up_p, wref, wpol_t, wpol_i)
 
 
 def per_device(
@@ -486,20 +550,20 @@
     mod = jnp.stack([ref_modality == 1, pol_modality == 1]).astype(f32)
     mod = jnp.concatenate([mod, jnp.zeros((6, rows), f32)], axis=0)
 
-    gate_r = ref_gate.T.astype(f32)
-    h_ref = (gate_r * jax.nn.sigmoid(gate_r) * ref_up.T.astype(f32)).astype(bf16)
-    gate_p, up_p = pol_gate.T.astype(f32), pol_up.T.astype(f32)
-    sig = jax.nn.sigmoid(gate_p)
-    act = gate_p * sig
-    h_pol = (act * up_p).astype(bf16)
     w_ref = jnp.concatenate([ref_down_text, ref_down_image], axis=1)
-    w_pol = jnp.concatenate([pol_down_text.T, pol_down_image.T], axis=1)
-
-    summed, d_hidden, grads = communicate(cot, mod, h_ref, w_ref, h_pol, w_pol)
+    summed, grad_gate, grad_up, grad_t, grad_i = communicate(
+        cot,
+        mod,
+        ref_gate.T,
+        ref_up.T,
+        pol_gate.T,
+        pol_up.T,
+        w_ref,
+        pol_down_text.T,
+        pol_down_image.T,
+    )
     ref_out = (summed.T.astype(f32) + ref_residual.astype(f32)).astype(bf16)
-    grad_gate = (d_hidden * up_p * sig * (1.0 + gate_p * (1.0 - sig))).astype(bf16)
-    grad_up = (d_hidden * act).astype(bf16)
-    return (ref_out, grad_gate.T, grad_up.T, grads[0].T, grads[1].T)
+    return (ref_out, grad_gate.T, grad_up.T, grad_t.T, grad_i.T)
 
 
 def solution(mesh):

time: 171 us -> 157 us (0.918)
  Pallas kernels: 151 us -> 143 us
  other arithmetic: 11.8 us -> 4.29 us
  local copies, waits for them, and re-layouts: 5.8 us -> 8.84 us
    pallas_call x1, Pallas kernels: 151 us -> 143 us  [communicate(): pl.pallas_call(step_kernel, out_shape=(jax.ShapeDtypeStruct((cols, rows),...]
    unnamed x33 -> x31, local copies, waits for them, and re-layouts: 1.87 us -> 8.67 us
    convert_element_type x1 -> x0, other arithmetic: 4.89 us -> none  [per_device(): h_pol = (act * up_p).astype(bf16)]
    transpose x1 -> x0, local copies, waits for them, and re-layouts: 3.75 us -> none  [per_device(): return (ref_out, grad_gate.T, grad_up.T, grads[0].T, grads[1].T)]
    transpose x1 -> x0, other arithmetic: 2.4 us -> none  [per_device(): return (ref_out, grad_gate.T, grad_up.T, grads[0].T, grads[1].T)]
where the time goes in v2:
time: 157 us
  Pallas kernels  143 us (91%)
  local copies, waits for them, and re-layouts  8.84 us (6%)
  other arithmetic  4.29 us (3%)
    pallas_call x1, Pallas kernels, communicate(): pl.pallas_call(step_kernel, out_shape=(jax.ShapeDtypeStruct((cols, rows),...  143 us
    unnamed x31, local copies, waits for them, and re-layouts  8.67 us

profile of v2, /device:TPU:2, one launch (start us, length us, event | category | flops | bytes accessed | tf_op | source)
XLA Modules:
  0.0 156.6 jit_solution(4037910451631829510)
XLA Ops:
  0.6 0.0 copy-start.4
  0.6 1.4 copy.30
  2.1 0.0 copy-done.4
  2.1 0.3 copy.31
  2.4 0.0 copy-start.5
  2.4 0.0 copy-start.10
  2.4 0.0 copy-start.9
  2.4 1.5 pad_maximum_fusion.wref_in
  4.0 0.0 copy-done.5
  4.0 0.0 copy-start.7
  4.0 0.0 copy-start.8
  4.0 0.2 copy.29
  4.1 0.0 copy-done.10
  4.2 0.1 broadcast_in_dim.28
  4.2 0.1 reshape.31
  4.3 0.0 copy-done.9
  4.3 0.1 select_reduce_fusion
  4.4 0.8 fusion.1.cot_in
  5.2 0.0 copy-done.7
  5.3 0.0 copy-done.8
  5.3 0.6 pad_convert_fusion.mod_in
  5.9 0.0 copy-start.6
  5.9 142.7 %shard_map.173 = (bf16[256,768]{1,0:T(8,128)(2,1)}, bf16[688,768]{1,0:T(8,128)(2,1)}, bf16[688,768]{1,0:T(8,128)(2,1)}, f32[688,512]{1,0:T(8,128)}, f32[688,512]{1,0:T(8,128)}) custom-call(bf16[256,768]{1,0:T(8,128)(2,1)} %fusion.1.cot_in, f32[8,768]{1,0:T(8,128)} %pad_convert_fusion.mod_in, bf16[688,768]{1,0:T(8,128)(2,1)} %bitcast.20, ...), custom_call_target="tpu_custom_call" | custom-call | tf_op jit(solution)/shard_map/pallas_call | solution.py:508
  148.6 0.0 copy-start.3
  148.6 0.0 copy-done.6
  148.6 0.2 copy.32
  148.8 1.2 fusion
  150.0 0.0 copy-start.2
  150.0 0.9 copy.33
  150.9 0.0 copy-done.3
  150.9 1.0 copy.38
  151.9 0.0 copy-done.2
  151.9 0.0 copy-start.1
  151.9 1.0 copy.39
  152.9 0.8 copy-done.1
  153.6 0.0 copy-start
  153.6 1.1 copy.40
  154.7 0.8 copy-done
  155.5 1.1 copy.41
  (7 shorter events, 0.1 us)
Async XLA Ops:
  0.6 1.5 copy-start.4
  2.4 1.6 %copy-start.5 = (bf16[768,256]{1,0:T(8,128)(2,1)S(1)}, bf16[768,256]{1,0:T(8,128)(2,1)}, u32[]{:S(2)}) copy-start(bf16[768,256]{1,0:T(8,128)(2,1)} %param.25) | copy-start | bytes 1179652
  2.4 1.8 %copy-start.10 = (f32[6]{0:T(128)S(1)}, f32[6]{0:T(128)}, u32[]{:S(2)}) copy-start(f32[6]{0:T(128)} %param.24) | copy-start | bytes 76
  2.4 1.9 %copy-start.9 = (s32[768]{0:T(1024)S(1)}, s32[768]{0:T(1024)}, u32[]{:S(2)}) copy-start(s32[768]{0:T(1024)} %param.23) | copy-start | bytes 9220
  4.0 1.3 copy-start.7
  4.0 1.3 copy-start.8
  5.9 142.7 %copy-start.6 = (bf16[768,256]{1,0:T(8,128)(2,1)S(1)}, bf16[768,256]{1,0:T(8,128)(2,1)}, u32[]{:S(2)}) copy-start(bf16[768,256]{1,0:T(8,128)(2,1)} %param.16) | copy-start | bytes 1179652
  148.6 2.3 %copy-start.3 = (bf16[688,768]{1,0:T(8,128)(2,1)S(1)}, bf16[688,768]{1,0:T(8,128)(2,1)}, u32[]{:S(2)}) copy-start(bf16[688,768]{1,0:T(8,128)(2,1)} %get-tuple-element.11) | copy-start | bytes 3170308
  150.0 1.9 %copy-start.2 = (bf16[688,768]{1,0:T(8,128)(2,1)S(1)}, bf16[688,768]{1,0:T(8,128)(2,1)}, u32[]{:S(2)}) copy-start(bf16[688,768]{1,0:T(8,128)(2,1)} %get-tuple-element.12) | copy-start | bytes 3170308
  151.9 1.7 %copy-start.1 = (f32[688,512]{1,0:T(8,128)S(1)}, f32[688,512]{1,0:T(8,128)}, u32[]{:S(2)}) copy-start(f32[688,512]{1,0:T(8,128)} %get-tuple-element.13) | copy-start | bytes 4227076
  153.6 1.9 %copy-start = (f32[688,512]{1,0:T(8,128)S(1)}, f32[688,512]{1,0:T(8,128)}, u32[]{:S(2)}) copy-start(f32[688,512]{1,0:T(8,128)} %get-tuple-element.14) | copy-start | bytes 4227076

commit v3 on v2

--- a/solution.py
+++ b/solution.py
@@ -27,25 +27,36 @@
 
 
 def step_kernel(
-    cot_in,
-    mod_in,
+    token_in,
+    ref_mod_in,
+    pol_mod_in,
+    segment_in,
+    margin_in,
     gate_r_in,
     up_r_in,
     gate_p_in,
     up_p_in,
-    wref_in,
+    wref_t_in,
+    wref_i_in,
     wpol_t_in,
     wpol_i_in,
     out_ref,
     out_gate,
     out_up,
-    out_t,
-    out_i,
+    own_t,
+    own_i,
+    far_t,
+    far_i,
+    dwo,
     gates,
     turned,
+    tokens,
+    cot_in,
+    mod_in,
     d_own,
     hr,
     hp,
+    wrt,
     wr,
     wp,
     cr,
@@ -69,7 +80,6 @@
     xa,
     xb,
     dws,
-    dwr,
     send_sems,
     recv_sems,
     local_sems,
@@ -79,7 +89,7 @@
     zl, x = fi // 4, fi % 4
     y, zh, c = ti // 4, (ti // 2) % 2, ti % 2
     ff, rows = gate_r_in.shape
-    cols = cot_in.shape[0]
+    cols = token_in.shape[1]
     cut = (ff // 32) * 16
     tiles = rows // 256
 
@@ -110,12 +120,13 @@
         here.start()
         return here
 
+    token_here = local(15, token_in, tokens)
     ref_here = [local(3, gate_r_in, gates.at[0]), local(4, up_r_in, gates.at[1])]
     depth = wpol_t_in.shape[1]
     pol_here = [local(5, gate_p_in, gates.at[2]), local(6, up_p_in, gates.at[3])]
     own = [
-        local(7, mod_in, mods.at[0]),
-        local(8, wref_in, wr.at[0]),
+        local(8, wref_t_in, wrt.at[0, 0]),
+        local(16, wref_i_in, wrt.at[0, 1]),
         local(9, wpol_t_in, wp.at[0, :, pl.ds(0, depth)]),
         local(10, wpol_i_in, wp.at[0, :, pl.ds(depth, depth)]),
     ]
@@ -142,6 +153,26 @@
 
         loop(ff // 16, chunk)
 
+    segment = segment_in[...].reshape(1, rows)
+    coef = jnp.zeros((1, rows), f32)
+    for p in range(margin_in.shape[0]):
+        margin = jnp.full((1, rows), margin_in[p], f32)
+        weight = dpo_beta * jax.nn.sigmoid(-dpo_beta * margin)
+        coef = jnp.where(segment == 2 * p, -weight, coef)
+        coef = jnp.where(segment == 2 * p + 1, weight, coef)
+    images = [(m[...].reshape(1, rows) == 1).astype(f32) for m in (ref_mod_in, pol_mod_in)]
+    for where in (mod_in, mods.at[0]):
+        for row, value in enumerate((*images, coef)):
+            where[pl.ds(row, 1)] = value
+        where[pl.ds(3, 5)] = jnp.zeros((5, rows), f32)
+    token_here.wait()
+
+    def weigh(n):
+        where = lanes(n)
+        turned_block = tokens[where, :].astype(f32).T
+        cot_in[:, where] = (turned_block * mods[0, pl.ds(2, 1), where]).astype(bf16)
+
+    loop(tiles, weigh)
     for here in ref_here:
         here.wait()
     hidden(0, hr)
@@ -214,17 +245,25 @@
         return copy(h.at[3, lo], h.at[2, lo], x_up), copy(h.at[1, hi], h.at[2, hi], x_down)
 
     h_up, h_down = spread_first(hr)
-    some = wref_in.shape[0] // 4
     w_far = []
 
-    def send_w(first, count):
-        where = pl.ds(first * some, count * some)
-        w_far.append(copy(wref_in.at[where], wr.at[1, where], zl_flip))
-
-    send_w(0, 2)
+    def send_w(modality, src, where):
+        w_far.append(copy(src.at[where], wrt.at[1, modality, where], zl_flip))
+
+    def flip(r, modality):
+        for first in range(0, ff, 128):
+            count = min(128, ff - first)
+            block = wrt[r, modality, pl.ds(first, count), :]
+            wr[r, modality, :, pl.ds(first, count)] = block.T
+
+    send_w(0, wref_t_in, pl.ds(0, ff))
     for here in pol_here:
         here.wait()
     hidden(2, hp)
+    for here in own:
+        here.wait()
+    flip(0, 0)
+    flip(0, 1)
 
     wait_turned()
     wait_moved = copy_or_stay(N_SEM + 2, turned, cr.at[c, k_own], shift_dev, shifts)
@@ -234,10 +273,8 @@
     p_up2, p_down2 = spread_last(hp)
     wait_moved()
     cot_zh = [copy(cr.at[c, k_own], cr.at[c, k_own], zh_flip)]
-    send_w(2, 1)
-    for here in own:
-        here.wait()
-    send_w(3, 1)
+    send_w(1, wref_i_in, lo)
+    send_w(1, wref_i_in, hi)
     wp_far = [
         copy(wpol_t_in, wp.at[1, :, pl.ds(0, depth)], zl_flip),
         copy(wpol_i_in, wp.at[1, :, pl.ds(depth, depth)], zl_flip),
@@ -262,14 +299,17 @@
             where = lanes(n)
             img = image(d, 0, where)
             block = hr[d, :, where]
-            hs[pl.ds(0, ff)] = block * (1 - img)
-            hs[pl.ds(ff, ff)] = block * img
+            hs[0] = block * (1 - img)
+            hs[1] = block * img
             for r in range(2):
                 there = pl.ds(pl.multiple_of((1 - c) * cols, cols), cols)
-                away = jnp.dot(wr[r, there], hs[...], preferred_element_type=f32)
+                away = jnp.dot(wr[r, 0, there], hs[0], preferred_element_type=f32)
+                away += jnp.dot(wr[r, 1, there], hs[1], preferred_element_type=f32)
                 aw[d, r, :, where] = away.astype(bf16)
                 stay = pl.ds(pl.multiple_of(c * cols, cols), cols)
-                kp[slot, r, :, where] = jnp.dot(wr[r, stay], hs[...], preferred_element_type=f32)
+                kept = jnp.dot(wr[r, 0, stay], hs[0], preferred_element_type=f32)
+                kept += jnp.dot(wr[r, 1, stay], hs[1], preferred_element_type=f32)
+                kp[slot, r, :, where] = kept
 
         loop(tiles, tile)
         return copy(aw.at[d], ar.at[d], c_flip)
@@ -285,8 +325,11 @@
 
         loop(tiles, tile)
 
-    for got in w_far:
-        got.wait_recv()
+    w_far[0].wait_recv()
+    flip(1, 0)
+    w_far[1].wait_recv()
+    w_far[2].wait_recv()
+    flip(1, 1)
     got0 = ref_piece(0, 0)
     p_opp_lo, p_opp_hi = pass_on(hp, p_up, p_down)
     got1 = ref_piece(1, 1)
@@ -357,17 +400,17 @@
 
     for got in cot_c:
         got.wait_recv()
+    p_up2.wait_recv()
+    p_down2.wait_recv()
+    p_opp_lo.wait_recv()
+    p_opp_hi.wait_recv()
+    away(0)
+    dw_sent = [copy(dws.at[0], far_t, zl_flip)]
     for got in wp_far:
         got.wait_recv()
     d_piece(2, store_dh(2))
     d_via_up = copy(dh.at[2, lo], xa_via, x_up)
     d_via_down = copy(dh.at[2, hi], xb_via, x_down)
-    p_up2.wait_recv()
-    p_down2.wait_recv()
-    p_opp_lo.wait_recv()
-    p_opp_hi.wait_recv()
-    away(0)
-    dw_sent = [copy(dws.at[0], dwr.at[0], zl_flip)]
     via_up.wait_recv()
     via_down.wait_recv()
 
@@ -414,7 +457,7 @@
     loop(tiles, add_d)
     d_last_up = copy(dh.at[0, lo], xa.at[lo], x_up)
     d_last_down = copy(dh.at[1, hi], xb.at[hi], x_down)
-    dw_sent.append(copy(dws.at[1], dwr.at[1], zl_flip))
+    dw_sent.append(copy(dws.at[1], far_i, zl_flip))
 
     def store_own(where, part):
         d_own[:, where] = part
@@ -426,17 +469,19 @@
 
     def z_sum(n):
         where = lanes(n)
-        fo[:, where] = (y_sum(zh, where) + zr[:, where].astype(f32)).astype(bf16)
+        fo[where, :] = (y_sum(zh, where) + zr[:, where].astype(f32)).T.astype(bf16)
 
     loop(tiles, z_sum)
     wait_back = copy_or_stay(N_SEM + 1, fo, out_ref, back_dev, moves)
 
-    for modality, out in enumerate((out_t, out_i)):
-
-        def column(core, modality=modality, out=out):
-            out[:, lanes(core)] = down(0, core, modality)
+    flushed = []
+    for modality, out in enumerate((own_t, own_i)):
+
+        def column(core, modality=modality):
+            dwo[modality, :, lanes(core)] = down(0, core, modality)
 
         loop(2, column)
+        flushed.append(local(11 + modality, dwo.at[modality], out))
 
     for got in (d_first_up, d_first_down, d_last_up, d_last_down):
         got.wait_recv()
@@ -446,40 +491,43 @@
         gate, up = gates[2, where].astype(f32), gates[3, where].astype(f32)
         d_hidden = d_own[where] + xa[where].astype(f32) + xb[where].astype(f32)
         sig = jax.nn.sigmoid(gate)
-        out_gate[where] = (d_hidden * up * sig * (1.0 + gate * (1.0 - sig))).astype(bf16)
-        out_up[where] = (d_hidden * (gate * sig)).astype(bf16)
+        gates[0, where] = (d_hidden * up * sig * (1.0 + gate * (1.0 - sig))).astype(bf16)
+        gates[1, where] = (d_hidden * (gate * sig)).astype(bf16)
 
     loop(ff // 16, d_sum)
-    for modality, out in enumerate((out_t, out_i)):
-        dw_sent[modality].wait_recv()
-
-        def dw_sum(core, modality=modality, out=out):
-            where = lanes(core)
-            out[:, where] = out[:, where] + dwr[modality, :, where].astype(f32)
-
-        loop(2, dw_sum)
+    flushed.append(local(13, gates.at[0], out_gate))
+    flushed.append(local(14, gates.at[1], out_up))
+    for got in dw_sent:
+        got.wait_recv()
+    for here in flushed:
+        here.wait()
     wait_back()
     for rdma in started:
         rdma.wait_send()
 
 
-def communicate(cot, mod, gate_r, up_r, gate_p, up_p, wref, wpol_t, wpol_i):
+def communicate(cot, ref_mod, pol_mod, segment, margin, gate_r, up_r, gate_p, up_p, wref_t, wref_i, wpol_t, wpol_i):
     ff, rows = gate_r.shape
-    cols = cot.shape[0]
-    depth = wref.shape[0]
+    cols = cot.shape[1]
+    depth = wref_t.shape[1]
     cut = (ff // 32) * 16
     vmem = pltpu.VMEM
     scratch = [
+        vmem((2, ff, depth), f32),
         vmem((4, ff, rows), bf16),
         vmem((cols, rows), bf16),
+        vmem((rows, cols), bf16),
+        vmem((cols, rows), bf16),
+        vmem((8, rows), f32),
         vmem((ff, rows), f32),
         vmem((4, ff, rows), bf16),
         vmem((4, ff, rows), bf16),
-        vmem((2, depth, 2 * ff), bf16),
+        vmem((2, 2, ff, depth), bf16),
+        vmem((2, 2, depth, ff), bf16),
         vmem((2, ff, 2 * depth), bf16),
         vmem((2, 8, cols, rows), bf16),
         vmem((4, 8, rows), f32),
-        vmem((2 * ff, 256), bf16),
+        vmem((2, ff, 256), bf16),
         vmem((8 * cols, 256), bf16),
         vmem((4, 2, cols, rows), bf16),
         vmem((4, 2, cols, rows), bf16),
@@ -491,36 +539,36 @@
         vmem((2, cols, rows), bf16),
         vmem((cols, rows), bf16),
         vmem((cols, rows), bf16),
-        vmem((cols, rows), bf16),
+        vmem((rows, cols), bf16),
         vmem((3, ff, rows), bf16),
         vmem((cut, rows), bf16),
         vmem((ff - cut, rows), bf16),
         vmem((ff, rows), bf16),
         vmem((ff, rows), bf16),
         vmem((2, ff, depth), bf16),
-        vmem((2, ff, depth), bf16),
         pltpu.SemaphoreType.DMA((N_SEM + 3,)),
         pltpu.SemaphoreType.DMA((N_SEM + 3,)),
-        pltpu.SemaphoreType.DMA((11,)),
+        pltpu.SemaphoreType.DMA((17,)),
     ]
     anywhere = pl.BlockSpec(memory_space=pl.ANY)
-    in_vmem = pl.BlockSpec(memory_space=vmem)
     return pl.pallas_call(
         step_kernel,
         out_shape=(
-            jax.ShapeDtypeStruct((cols, rows), bf16),
+            jax.ShapeDtypeStruct((rows, cols), bf16),
             jax.ShapeDtypeStruct((ff, rows), bf16),
             jax.ShapeDtypeStruct((ff, rows), bf16),
             jax.ShapeDtypeStruct((ff, depth), f32),
             jax.ShapeDtypeStruct((ff, depth), f32),
+            jax.ShapeDtypeStruct((ff, depth), bf16),
+            jax.ShapeDtypeStruct((ff, depth), bf16),
         ),
-        in_specs=[anywhere] * 9,
-        out_specs=(in_vmem,) * 5,
+        in_specs=[anywhere] + [pl.BlockSpec(memory_space=vmem)] * 3 + [pl.BlockSpec(memory_space=pltpu.SMEM)] + [anywhere] * 8,
+        out_specs=(anywhere,) * 7,
         scratch_shapes=scratch,
         compiler_params=pltpu.CompilerParams(
             collective_id=0, has_side_effects=True, vmem_limit_bytes=66_000_000
         ),
-    )(cot, mod, gate_r, up_r, gate_p, up_p, wref, wpol_t, wpol_i)
+    )(cot, ref_mod, pol_mod, segment, margin, gate_r, up_r, gate_p, up_p, wref_t, wref_i, wpol_t, wpol_i)
 
 
 def per_device(
@@ -540,29 +588,24 @@
     pol_down_image,
 ):
     rows = ref_gate.shape[0]
-    seg_ids = jnp.arange(2 * pair_margin.shape[0], dtype=jnp.int32)
-    pair_weight = dpo_beta * jax.nn.sigmoid(-dpo_beta * pair_margin)
-    table = jnp.repeat(pair_weight, 2) * jnp.where(seg_ids % 2 == 0, -1.0, 1.0).astype(f32)
-    coef = jnp.sum(
-        jnp.where(pol_segment[None, :] == seg_ids[:, None], table[:, None], f32(0.0)), axis=0
-    )
-    cot = (coef[None, :] * token_cotangent.T.astype(f32)).astype(bf16)
-    mod = jnp.stack([ref_modality == 1, pol_modality == 1]).astype(f32)
-    mod = jnp.concatenate([mod, jnp.zeros((6, rows), f32)], axis=0)
-
-    w_ref = jnp.concatenate([ref_down_text, ref_down_image], axis=1)
-    summed, grad_gate, grad_up, grad_t, grad_i = communicate(
-        cot,
-        mod,
+    summed, grad_gate, grad_up, own_t, own_i, far_t, far_i = communicate(
+        token_cotangent,
+        ref_modality,
+        pol_modality,
+        pol_segment,
+        pair_margin,
         ref_gate.T,
         ref_up.T,
         pol_gate.T,
         pol_up.T,
-        w_ref,
+        ref_down_text.T,
+        ref_down_image.T,
         pol_down_text.T,
         pol_down_image.T,
     )
-    ref_out = (summed.T.astype(f32) + ref_residual.astype(f32)).astype(bf16)
+    ref_out = (summed.astype(f32) + ref_residual.astype(f32)).astype(bf16)
+    grad_t = own_t + far_t.astype(f32)
+    grad_i = own_i + far_i.astype(f32)
     return (ref_out, grad_gate.T, grad_up.T, grad_t.T, grad_i.T)
 
 

time: 157 us -> 150 us (0.955)
  local copies, waits for them, and re-layouts: 8.84 us -> 2.59 us
  Pallas kernels: 143 us -> 140 us
  other arithmetic: 4.29 us -> 6.07 us
    unnamed x31 -> x10, local copies, waits for them, and re-layouts: 8.67 us -> 2.59 us
    transpose x0 -> x1, other arithmetic: none -> 4.16 us  [per_device(): return (ref_out, grad_gate.T, grad_up.T, grad_t.T, grad_i.T)]
    pallas_call x1, Pallas kernels: 143 us -> 140 us  [communicate(): pl.pallas_call(step_kernel, out_shape=(jax.ShapeDtypeStruct((rows, cols),...]
    concatenate x2 -> x0, other arithmetic: 2.16 us -> none  [the longest x1 1.55 us: per_device(): w_ref = jnp.concatenate([ref_down_text, ref_down_image], axis=1)]
where the time goes in v3:
time: 150 us
  Pallas kernels  140 us (93%)
  other arithmetic  6.07 us (4%)
  local copies, waits for them, and re-layouts  2.59 us (2%)
    pallas_call x1, Pallas kernels, communicate(): pl.pallas_call(step_kernel, out_shape=(jax.ShapeDtypeStruct((rows, cols),...  140 us
    transpose x1, other arithmetic, per_device(): return (ref_out, grad_gate.T, grad_up.T, grad_t.T, grad_i.T)  4.16 us

profile of v3, /device:TPU:2, one launch (start us, length us, event | category | flops | bytes accessed | tf_op | source)
XLA Modules:
  0.0 149.7 jit_solution(14127669969363659726)
XLA Ops:
  0.6 0.0 copy-start.3
  0.6 140.3 %shard_map.173 = (bf16[768,256]{1,0:T(8,128)(2,1)}, bf16[688,768]{1,0:T(8,128)(2,1)}, bf16[688,768]{1,0:T(8,128)(2,1)}, f32[688,512]{1,0:T(8,128)}, f32[688,512]...) custom-call(bf16[768,256]{1,0:T(8,128)(2,1)} %token_in.1, s32[768]{0:T(1024)} %ref_mod_in.1, ...), custom_call_target="tpu_custom_call" | custom-call | tf_op jit(solution)/shard_map/pallas_call | solution.py:554
  141.0 0.0 copy-start.2
  141.0 0.0 copy-done.3
  141.0 1.9 %add_convert_fusion = bf16[768,256]{1,0:T(8,128)(2,1)} fusion(bf16[768,256]{1,0:T(8,128)(2,1)S(1)} %copy-done.3, bf16[768,256]{1,0:T(8,128)(2,1)} %get-tuple-element.12), kind=kLoop, calls=%fused_computation.2 | loop fusion | flops 786432 | bytes 1179648 | tf_op jit(solution)/shard_map/convert_element_type | solution.py:606
  142.9 0.0 copy-done.2
  142.9 0.0 copy-start.1
  142.9 4.2 %add_bitcast_fusion = (f32[512,688]{0,1:T(8,128)}, f32[512,688]{0,1:T(8,128)}) fusion(f32[688,512]{1,0:T(8,128)} %get-tuple-element.17, bf16[688,512]{1,0:T(8,128)(2,1)} %get-tuple-element.18, f32[688,512]{1,0:T(8,128)} %get-tuple-element.15, bf16[688,512]{1,0:T(8,128)(2,1)S(1)} %copy-done.2), kind=kLoop, calls=%fused_computation | loop fusion | flops 1409024 | bytes 7045120 | tf_op jit(solution)/shard_map/transpose | solution.py:609
  147.1 0.0 copy-start
  147.1 0.0 copy-done.1
  147.1 1.0 copy.21
  148.0 0.6 copy-done
  148.7 1.0 copy.22
Async XLA Ops:
  0.6 140.3 %copy-start.3 = (bf16[768,256]{1,0:T(8,128)(2,1)S(1)}, bf16[768,256]{1,0:T(8,128)(2,1)}, u32[]{:S(2)}) copy-start(bf16[768,256]{1,0:T(8,128)(2,1)} %param.16) | copy-start | bytes 1179652
  141.0 1.9 %copy-start.2 = (bf16[688,512]{1,0:T(8,128)(2,1)S(1)}, bf16[688,512]{1,0:T(8,128)(2,1)}, u32[]{:S(2)}) copy-start(bf16[688,512]{1,0:T(8,128)(2,1)} %get-tuple-element.16) | copy-start | bytes 2113540
  142.9 4.2 %copy-start.1 = (bf16[688,768]{1,0:T(8,128)(2,1)S(1)}, bf16[688,768]{1,0:T(8,128)(2,1)}, u32[]{:S(2)}) copy-start(bf16[688,768]{1,0:T(8,128)(2,1)} %get-tuple-element.13) | copy-start | bytes 3170308
  147.1 1.6 %copy-start = (bf16[688,768]{1,0:T(8,128)(2,1)S(1)}, bf16[688,768]{1,0:T(8,128)(2,1)}, u32[]{:S(2)}) copy-start(bf16[688,768]{1,0:T(8,128)(2,1)} %get-tuple-element.14) | copy-start | bytes 3170308

commit v4 on v3

--- a/solution.py
+++ b/solution.py
@@ -28,6 +28,7 @@
 
 def step_kernel(
     token_in,
+    residual_in,
     ref_mod_in,
     pol_mod_in,
     segment_in,
@@ -51,6 +52,8 @@
     gates,
     turned,
     tokens,
+    residual,
+    landed,
     cot_in,
     mod_in,
     d_own,
@@ -125,6 +128,7 @@
     depth = wpol_t_in.shape[1]
     pol_here = [local(5, gate_p_in, gates.at[2]), local(6, up_p_in, gates.at[3])]
     own = [
+        local(17, residual_in, residual),
         local(8, wref_t_in, wrt.at[0, 0]),
         local(16, wref_i_in, wrt.at[0, 1]),
         local(9, wpol_t_in, wp.at[0, :, pl.ds(0, depth)]),
@@ -472,7 +476,7 @@
         fo[where, :] = (y_sum(zh, where) + zr[:, where].astype(f32)).T.astype(bf16)
 
     loop(tiles, z_sum)
-    wait_back = copy_or_stay(N_SEM + 1, fo, out_ref, back_dev, moves)
+    wait_back = copy_or_stay(N_SEM + 1, fo, landed, back_dev, moves)
 
     flushed = []
     for modality, out in enumerate((own_t, own_i)):
@@ -497,16 +501,24 @@
     loop(ff // 16, d_sum)
     flushed.append(local(13, gates.at[0], out_gate))
     flushed.append(local(14, gates.at[1], out_up))
+    wait_back()
+
+    def add_residual(n):
+        where = lanes(n)
+        total = landed[where, :].astype(f32) + residual[where, :].astype(f32)
+        residual[where, :] = total.astype(bf16)
+
+    loop(tiles, add_residual)
+    flushed.append(local(18, residual, out_ref))
     for got in dw_sent:
         got.wait_recv()
     for here in flushed:
         here.wait()
-    wait_back()
     for rdma in started:
         rdma.wait_send()
 
 
-def communicate(cot, ref_mod, pol_mod, segment, margin, gate_r, up_r, gate_p, up_p, wref_t, wref_i, wpol_t, wpol_i):
+def communicate(cot, resid, ref_mod, pol_mod, segment, margin, gate_r, up_r, gate_p, up_p, wref_t, wref_i, wpol_t, wpol_i):
     ff, rows = gate_r.shape
     cols = cot.shape[1]
     depth = wref_t.shape[1]
@@ -516,6 +528,8 @@
         vmem((2, ff, depth), f32),
         vmem((4, ff, rows), bf16),
         vmem((cols, rows), bf16),
+        vmem((rows, cols), bf16),
+        vmem((rows, cols), bf16),
         vmem((rows, cols), bf16),
         vmem((cols, rows), bf16),
         vmem((8, rows), f32),
@@ -548,7 +562,7 @@
         vmem((2, ff, depth), bf16),
         pltpu.SemaphoreType.DMA((N_SEM + 3,)),
         pltpu.SemaphoreType.DMA((N_SEM + 3,)),
-        pltpu.SemaphoreType.DMA((17,)),
+        pltpu.SemaphoreType.DMA((19,)),
     ]
     anywhere = pl.BlockSpec(memory_space=pl.ANY)
     return pl.pallas_call(
@@ -562,13 +576,13 @@
             jax.ShapeDtypeStruct((ff, depth), bf16),
             jax.ShapeDtypeStruct((ff, depth), bf16),
         ),
-        in_specs=[anywhere] + [pl.BlockSpec(memory_space=vmem)] * 3 + [pl.BlockSpec(memory_space=pltpu.SMEM)] + [anywhere] * 8,
+        in_specs=[anywhere] * 2 + [pl.BlockSpec(memory_space=vmem)] * 3 + [pl.BlockSpec(memory_space=pltpu.SMEM)] + [anywhere] * 8,
         out_specs=(anywhere,) * 7,
         scratch_shapes=scratch,
         compiler_params=pltpu.CompilerParams(
             collective_id=0, has_side_effects=True, vmem_limit_bytes=66_000_000
         ),
-    )(cot, ref_mod, pol_mod, segment, margin, gate_r, up_r, gate_p, up_p, wref_t, wref_i, wpol_t, wpol_i)
+    )(cot, resid, ref_mod, pol_mod, segment, margin, gate_r, up_r, gate_p, up_p, wref_t, wref_i, wpol_t, wpol_i)
 
 
 def per_device(
@@ -588,8 +602,9 @@
     pol_down_image,
 ):
     rows = ref_gate.shape[0]
-    summed, grad_gate, grad_up, own_t, own_i, far_t, far_i = communicate(
+    ref_out, grad_gate, grad_up, own_t, own_i, far_t, far_i = communicate(
         token_cotangent,
+        ref_residual,
         ref_modality,
         pol_modality,
         pol_segment,
@@ -603,7 +618,6 @@
         pol_down_text.T,
         pol_down_image.T,
     )
-    ref_out = (summed.astype(f32) + ref_residual.astype(f32)).astype(bf16)
     grad_t = own_t + far_t.astype(f32)
     grad_i = own_i + far_i.astype(f32)
     return (ref_out, grad_gate.T, grad_up.T, grad_t.T, grad_i.T)

time: 150 us -> 148 us (0.987)
  other arithmetic: 6.07 us -> 4.32 us
    convert_element_type x1 -> x0, other arithmetic: 1.92 us -> none  [per_device(): ref_out = (summed.astype(f32) + ref_residual.astype(f32)).astype(bf16)]
where the time goes in v4:
time: 148 us
  Pallas kernels  140 us (95%)
  other arithmetic  4.32 us (3%)
  local copies, waits for them, and re-layouts  2.7 us (2%)
    pallas_call x1, Pallas kernels, communicate(): pl.pallas_call(step_kernel, out_shape=(jax.ShapeDtypeStruct((rows, cols),...  140 us
    transpose x1, other arithmetic, per_device(): return (ref_out, grad_gate.T, grad_up.T, grad_t.T, grad_i.T)  4.32 us

profile of v4, /device:TPU:2, one launch (start us, length us, event | category | flops | bytes accessed | tf_op | source)
XLA Modules:
  0.0 148.0 jit_solution(1730643456309762646)
XLA Ops:
  0.6 140.3 %shard_map.173 = (bf16[768,256]{1,0:T(8,128)(2,1)}, bf16[688,768]{1,0:T(8,128)(2,1)}, bf16[688,768]{1,0:T(8,128)(2,1)}, f32[688,512]{1,0:T(8,128)}, f32[688,512]...) custom-call(bf16[768,256]{1,0:T(8,128)(2,1)} %token_in.1, bf16[768,256]{1,0:T(8,128)(2,1)} %residual_in.1, ...), custom_call_target="tpu_custom_call" | custom-call | tf_op jit(solution)/shard_map/pallas_call | solution.py:568
  140.9 0.0 copy-start.2
  140.9 0.0 copy-start.1
  140.9 4.3 %add_bitcast_fusion = (f32[512,688]{0,1:T(8,128)}, f32[512,688]{0,1:T(8,128)}) fusion(f32[688,512]{1,0:T(8,128)} %get-tuple-element.17, bf16[688,512]{1,0:T(8,128)(2,1)} %get-tuple-element.18, f32[688,512]{1,0:T(8,128)} %get-tuple-element.15, bf16[688,512]{1,0:T(8,128)(2,1)} %get-tuple-element.16), kind=kLoop, calls=%fused_computation | loop fusion | flops 1409024 | bytes 7045120 | tf_op jit(solution)/shard_map/transpose | solution.py:623
  145.3 0.0 copy-done.2
  145.3 0.0 copy-start
  145.3 0.7 copy.22
  146.0 0.0 copy-done.1
  146.0 1.0 copy.23
  147.0 0.0 copy-done
  147.0 1.0 copy.24
Async XLA Ops:
  140.9 4.3 %copy-start.2 = (bf16[768,256]{1,0:T(8,128)(2,1)S(1)}, bf16[768,256]{1,0:T(8,128)(2,1)}, u32[]{:S(2)}) copy-start(bf16[768,256]{1,0:T(8,128)(2,1)} %get-tuple-element.26) | copy-start | bytes 1179652
  140.9 5.1 %copy-start.1 = (bf16[688,768]{1,0:T(8,128)(2,1)S(1)}, bf16[688,768]{1,0:T(8,128)(2,1)}, u32[]{:S(2)}) copy-start(bf16[688,768]{1,0:T(8,128)(2,1)} %get-tuple-element.13) | copy-start | bytes 3170308
  145.3 1.7 %copy-start = (bf16[688,768]{1,0:T(8,128)(2,1)S(1)}, bf16[688,768]{1,0:T(8,128)(2,1)}, u32[]{:S(2)}) copy-start(bf16[688,768]{1,0:T(8,128)(2,1)} %get-tuple-element.14) | copy-start | bytes 3170308
